TPU v7x, 32 devices: a whole 2x2x4 slice. The times are simulated.
32 devices in a mesh: groups: 2 (over y), dp: 4 (over z), rep: 4 (over x, core).
Axes of the slice: x: 2, y: 2, z: 4, core: 2. Of those that a mesh axis runs over, the one named last changes fastest.
Arguments:
- latent_store: bfloat16 [8, 48, 576, 128], P(('groups', 'dp'), 'rep'), parts along dimension 0, may hold values from -6 to 6
- page_rank: int32 [8, 48], P('groups', 'rep'), parts along dimension 0, may hold values from 0 to 3, as said below
- page_index: int32 [8, 48], P('groups', 'rep'), parts along dimension 0, may hold values from 0 to 11, as said below
- lengths: int32 [8, 1], P('groups'), parts along dimension 0, may hold values from 1536 to 6144, as said below
- queries: bfloat16 [16, 36864], P(('groups', 'dp')), parts along dimension 0, may hold values from -250 to 250
- new_latent: bfloat16 [16, 576], P(('groups', 'dp')), parts along dimension 0, may hold values from -4 to 4
- up_value: bfloat16 [64, 512, 128], P('dp'), may hold values from -0.25 to 0.25
- out_proj: bfloat16 [8192, 7168], P('dp', 'rep'), may hold values from -0.0625 to 0.0625
- residual: bfloat16 [16, 7168], P(('groups', 'dp'), 'rep'), parts along dimension 0, may hold values from -11 to 11
- norm_gain: float32 [7168], P('rep'), may hold values from 0.1 to 1.9
- w_gate: bfloat16 [7168, 12288], P('rep', 'dp'), may hold values from -0.0625 to 0.0625
- w_up: bfloat16 [7168, 12288], P('rep', 'dp'), may hold values from -0.0625 to 0.0625
- w_down: bfloat16 [12288, 7168], P('dp', 'rep'), may hold values from -0.0546875 to 0.0546875
Outputs:
- layer_out: bfloat16 [16, 7168], P(('groups', 'dp'), 'rep'), parts along dimension 0
There are 2 independent parts, one for each index of `groups`. A program takes and returns all parts, laid end to end along the dimension named above; an argument that names none is the same for every part. Nothing has to cross between parts.
Inputs may be any that keep to these rules, and one draw needn't show every extreme that they name: page_rank[d, q] is the storage rank holding slot q of rank d, on its device with rep index q // 12; one storage device holds at most 3 slot of one rank, and some holds exactly 3. page_index[d, q] is the slot's page among the 12 pages of its storage device; over all ranks every page of every storage device is named by exactly one slot. `lengths`: some request has exactly 6144 tokens.
All inputs are finite; a program needn't handle non-finite values.
Results may differ from a plain program's by a relative error of at most 0.015.
Values may be sent and summed in bfloat16 or wider, within the bound.
A program may use at most 128 MiB of HBM per device.

v0:
```python
import functools
import math

import jax
import jax.numpy as jnp
from jax import lax
from jax.experimental import pallas as pl
from jax.experimental.pallas import tpu as pltpu
from jax.sharding import PartitionSpec as P

D = 7168
CKV = 512
PAGE = 128
PAGES = 48


score_scale = 1.0 / math.sqrt(192.0)
epsilon = 1e-06
mask_value = -1e30


MESH = pl.DeviceIdType.MESH


def tile_of(width):
    for tile in (512, 256, 128):
        if width % tile == 0:
            return tile
    return width


def layer_kernel(
    dp,
    rep,
    query_ref,
    fresh_ref,
    bias_ref,
    residual_ref,
    gain_ref,
    store_hbm,
    up_value_hbm,
    out_proj_hbm,
    w_gate_hbm,
    w_up_hbm,
    w_down_hbm,
    out_ref,
    pages,
    queries,
    scores,
    part,
    part_stat,
    part_recv,
    stat_recv,
    share,
    share_stat,
    share_recv,
    share_stat_recv,
    value_buf,
    up_value,
    out_proj,
    w_gate,
    w_up,
    w_down,
    values,
    res_buf,
    op_buf,
    mixed,
    scaled,
    sq_buf,
    gu_buf,
    hidden,
    down_send,
    down_recv,
    weight_sem,
    q_send,
    q_recv,
    f_send,
    f_recv,
    p_send,
    p_recv,
    s_send,
    s_recv,
    v_send,
    v_recv,
    res_send,
    res_recv,
    op_send,
    op_recv,
    sq_send,
    sq_recv,
    gu_send,
    gu_recv,
    dn_send,
    dn_recv,
):
    my_rank = lax.axis_index("dp")
    my_column = lax.axis_index("rep")
    weights = []
    for i, (source, target) in enumerate(
        (
            (store_hbm.at[0], pages),
            (up_value_hbm, up_value),
            (out_proj_hbm, out_proj),
            (w_gate_hbm, w_gate),
            (w_up_hbm, w_up),
            (w_down_hbm, w_down),
        )
    ):
        copy = pltpu.make_async_copy(source, target, weight_sem.at[i])
        copy.start()
        weights.append(copy)

    barrier = pltpu.get_barrier_semaphore()
    ranks = [lax.rem(my_rank + k, dp) for k in range(1, dp)]
    columns = [lax.rem(my_column + k, rep) for k in range(1, rep)]
    for peer in ranks:
        pl.semaphore_signal(barrier, inc=1, device_id={"dp": peer}, device_id_type=MESH)
    for peer in columns:
        pl.semaphore_signal(barrier, inc=1, device_id={"rep": peer}, device_id_type=MESH)
    pl.semaphore_wait(barrier, dp - 1 + rep - 1)

    def to(axis, peer, source, target, send, recv):
        return pltpu.make_async_remote_copy(
            src_ref=source,
            dst_ref=target,
            send_sem=send,
            recv_sem=recv,
            device_id={axis: peer},
            device_id_type=MESH,
        )

    def spread(axis, source, target, send, recv):
        peers = ranks if axis == "dp" else columns
        copies = [
            to(axis, peer, source, target, send.at[k], recv.at[k]) for k, peer in enumerate(peers)
        ]
        for copy in copies:
            copy.start()
        return copies

    res_copies = spread("dp", residual_ref, res_buf.at[my_rank], res_send, res_recv)
    res_buf[my_rank] = residual_ref[...]

    q_copies = spread("dp", query_ref.at[my_column], queries.at[my_rank, my_column], q_send, q_recv)
    queries[my_rank] = query_ref[...]
    f_copies = []
    for k, copy in enumerate(q_copies):
        copy.wait()
        block = queries.at[lax.rem(my_rank + dp - 1 - k, dp), my_column]
        f_copies.append(spread("rep", block, block, f_send.at[k], f_recv.at[k]))
    for copies in f_copies:
        for copy in copies:
            copy.wait()

    rows_here, width = residual_ref.shape
    rows = dp * rows_here
    page_count, latent_width, page = pages.shape
    query_count = rep * query_ref.shape[1]
    group = dp // rep
    share_rows = query_count // dp
    weights[0].wait()
    row_ids = lax.broadcasted_iota(jnp.int32, (query_count, 1), 0) % rows_here
    lanes = lax.broadcasted_iota(jnp.int32, (query_count, 128), 1)

    def attend(d, carry):
        query = queries[d].reshape(query_count, latent_width)
        for p in range(page_count + 1):
            keys = pages[p] if p < page_count else fresh_ref[...]
            scores[:, p * page : (p + 1) * page] = jnp.dot(
                query, keys, preferred_element_type=jnp.float32
            )
        bias = bias_ref[d]
        limit = bias[0:1]
        for r in range(1, rows_here):
            limit = jnp.where(row_ids == r, bias[r : r + 1], limit)
        visible = limit > 0.5
        score = jnp.where(visible, scores[...] * score_scale, mask_value)
        peak = jnp.max(score, axis=1, keepdims=True)
        weight = jnp.where(visible, jnp.exp(score - peak), 0.0)
        total = jnp.sum(weight, axis=1, keepdims=True)
        weight = weight.astype(jnp.bfloat16)
        value = jnp.zeros((query_count, CKV), jnp.float32)
        for p in range(page_count + 1):
            keys = pages[p, :CKV] if p < page_count else fresh_ref[:CKV]
            value += lax.dot_general(
                weight[:, p * page : (p + 1) * page],
                keys,
                (((1,), (1,)), ((), ())),
                preferred_element_type=jnp.float32,
            )
        part[d // group, d % group] = value.astype(jnp.bfloat16)
        both = jnp.where(lanes % 2 == 0, peak, total)
        part_stat[d // group, d % group] = both.T[:8]
        return carry

    lax.fori_loop(0, dp, attend, 0)

    p_copies = []
    for k, peer in enumerate(columns):
        for j, (source, target) in enumerate(((part, part_recv), (part_stat, stat_recv))):
            copy = to(
                "rep",
                peer,
                source.at[peer],
                target.at[my_column],
                p_send.at[j, k],
                p_recv.at[j, k],
            )
            copy.start()
            p_copies.append(copy)
    part_recv[my_column] = part[my_column]
    stat_recv[my_column] = part_stat[my_column]
    for copy in p_copies:
        copy.wait()
    for g in range(group):
        peaks, totals = [], []
        for c in range(rep):
            stat = stat_recv[c, g]
            peaks.append(jnp.broadcast_to(stat[0:1], (128, query_count)).T[:, :1])
            totals.append(jnp.broadcast_to(stat[1:2], (128, query_count)).T[:, :1])
        best = functools.reduce(jnp.maximum, peaks)
        value = jnp.zeros((query_count, CKV), jnp.float32)
        total = jnp.zeros((query_count, 1), jnp.float32)
        for c in range(rep):
            factor = jnp.exp(peaks[c] - best)
            value += part_recv[c, g].astype(jnp.float32) * factor
            total += totals[c] * factor
        value = value.astype(jnp.bfloat16)
        both = jnp.where(lanes % 2 == 0, best, total)
        for p in range(dp):
            share[p, g] = value[p * share_rows : (p + 1) * share_rows]
            share_stat[p, g] = both[p * share_rows : (p + 1) * share_rows]

    s_copies = []
    for k, peer in enumerate(ranks):
        for j, (source, target) in enumerate(((share, share_recv), (share_stat, share_stat_recv))):
            copy = to(
                "dp",
                peer,
                source.at[peer],
                target.at[my_rank],
                s_send.at[j, k],
                s_recv.at[j, k],
            )
            copy.start()
            s_copies.append(copy)
    share_recv[my_rank] = share[my_rank]
    share_stat_recv[my_rank] = share_stat[my_rank]
    for copy in s_copies:
        copy.wait()
    heads = up_value.shape[0]
    vdim = up_value.shape[2]
    weights[1].wait()
    for g in range(group):
        best = share_stat_recv[0, g][:, 0:1]
        for p in range(1, dp):
            best = jnp.maximum(best, share_stat_recv[p, g][:, 0:1])
        value = jnp.zeros((share_rows, CKV), jnp.float32)
        total = jnp.zeros((share_rows, 1), jnp.float32)
        for p in range(dp):
            factor = jnp.exp(share_stat_recv[p, g][:, 0:1] - best)
            value += share_recv[p, g].astype(jnp.float32) * factor
            total += share_stat_recv[p, g][:, 1:2] * factor
        latent = (value / total).astype(jnp.bfloat16)
        for h in range(heads):
            value_buf[my_column, g, :, h * vdim : (h + 1) * vdim] = jnp.dot(
                latent[h * rows_here : (h + 1) * rows_here],
                up_value[h],
                preferred_element_type=jnp.float32,
            ).astype(jnp.bfloat16)
    for copy in spread(
        "rep", value_buf.at[my_column], value_buf.at[my_column], v_send, v_recv
    ):
        copy.wait()
    values[...] = jnp.concatenate(
        [value_buf[c, g].astype(jnp.float32) for c in range(rep) for g in range(group)], axis=0
    ).astype(jnp.bfloat16)

    weights[2].wait()
    tile = tile_of(width)

    def project(i, carry):
        at = pl.ds(pl.multiple_of(i * tile, tile), tile)
        op_buf[my_rank, :, at] = jnp.dot(
            values[...], out_proj[:, at], preferred_element_type=jnp.float32
        ).astype(jnp.bfloat16)
        return carry

    lax.fori_loop(0, width // tile, project, 0)
    op_copies = spread("dp", op_buf.at[my_rank], op_buf.at[my_rank], op_send, op_recv)
    for copy in res_copies:
        copy.wait()
    for copy in op_copies:
        copy.wait()
    attn_out = op_buf[0].astype(jnp.float32)
    for source in range(1, dp):
        attn_out += op_buf[source].astype(jnp.float32)
    squares = []
    for source in range(dp):
        part = attn_out[source * rows_here : (source + 1) * rows_here]
        mixed[source] = res_buf[source].astype(jnp.float32) + part
    whole = jnp.concatenate([mixed[source] for source in range(dp)], axis=0)
    squares = jnp.sum(whole * whole, axis=1, keepdims=True)
    sq_buf[my_column] = jnp.broadcast_to(squares, (rows, 128))
    sq_copies = spread("rep", sq_buf.at[my_column], sq_buf.at[my_column], sq_send, sq_recv)
    scaled[...] = (whole * gain_ref[...]).astype(jnp.bfloat16)

    chunks, chunk = gu_buf.shape[1], gu_buf.shape[4]
    step = tile_of(chunk)
    weights[3].wait()
    weights[4].wait()
    gu_copies = []
    for c in range(chunks):

        def gate_up(i, carry):
            at = pl.ds(pl.multiple_of(i * step, step), step)
            source = pl.ds(pl.multiple_of(c * chunk + i * step, step), step)
            gu_buf[my_column, c, 0, :, at] = jnp.dot(
                scaled[...], w_gate[:, source], preferred_element_type=jnp.float32
            ).astype(jnp.bfloat16)
            gu_buf[my_column, c, 1, :, at] = jnp.dot(
                scaled[...], w_up[:, source], preferred_element_type=jnp.float32
            ).astype(jnp.bfloat16)
            return carry

        lax.fori_loop(0, chunk // step, gate_up, 0)
        block = gu_buf.at[my_column, c]
        gu_copies.append(spread("rep", block, block, gu_send.at[c], gu_recv.at[c]))

    for copy in sq_copies:
        copy.wait()
    total = sq_buf[0]
    for source in range(1, rep):
        total += sq_buf[source]
    scale = lax.rsqrt(total[:, :1] / D + epsilon)
    for c in range(chunks):
        for copy in gu_copies[c]:
            copy.wait()
        gate = gu_buf[0, c, 0].astype(jnp.float32)
        up = gu_buf[0, c, 1].astype(jnp.float32)
        for source in range(1, rep):
            gate += gu_buf[source, c, 0].astype(jnp.float32)
            up += gu_buf[source, c, 1].astype(jnp.float32)
        gate = gate * scale
        up = up * scale
        hidden[:, c * chunk : (c + 1) * chunk] = (gate / (1.0 + jnp.exp(-gate)) * up).astype(
            jnp.bfloat16
        )

    weights[5].wait()

    def project_down(i, carry):
        at = pl.ds(pl.multiple_of(i * tile, tile), tile)
        part = jnp.dot(hidden[...], w_down[:, at], preferred_element_type=jnp.float32).astype(
            jnp.bfloat16
        )
        for p in range(dp):
            down_send[p, :, at] = part[p * rows_here : (p + 1) * rows_here]
        return carry

    lax.fori_loop(0, width // tile, project_down, 0)
    dn_copies = [
        to("dp", peer, down_send.at[peer], down_recv.at[my_rank], dn_send.at[k], dn_recv.at[k])
        for k, peer in enumerate(ranks)
    ]
    for copy in dn_copies:
        copy.start()
    result = mixed[my_rank] + down_send[my_rank].astype(jnp.float32)
    for copy in dn_copies:
        copy.wait()
    for peer in ranks:
        result += down_recv[peer].astype(jnp.float32)
    out_ref[...] = result.astype(jnp.bfloat16)


def layer(
    query_rows,
    fresh_page,
    bias,
    residual,
    norm_gain,
    latent_store,
    up_value,
    out_proj,
    w_gate,
    w_up,
    w_down,
):
    dp, rep = lax.axis_size("dp"), lax.axis_size("rep")
    rows_here, width = residual.shape
    rows = dp * rows_here
    inner, hidden_width = out_proj.shape[0], w_gate.shape[1]
    group = dp // rep
    query_count = rep * query_rows.shape[1]
    share_rows = query_count // dp
    chunks = 3 if hidden_width % (3 * 128) == 0 else 1
    bf16, f32 = jnp.bfloat16, jnp.float32
    dma = pltpu.SemaphoreType.DMA
    vmem = pl.BlockSpec(memory_space=pltpu.VMEM)
    hbm = pl.BlockSpec(memory_space=pl.ANY)
    return pl.pallas_call(
        functools.partial(layer_kernel, dp, rep),
        out_shape=jax.ShapeDtypeStruct((rows_here, width), bf16),
        in_specs=[vmem] * 5 + [hbm] * 6,
        out_specs=vmem,
        scratch_shapes=[
            pltpu.VMEM(latent_store.shape[1:], bf16),
            pltpu.VMEM((dp,) + query_rows.shape, bf16),
            pltpu.VMEM((query_count, bias.shape[2]), f32),
            pltpu.VMEM((rep, group, query_count, CKV), bf16),
            pltpu.VMEM((rep, group, 8, query_count), f32),
            pltpu.VMEM((rep, group, query_count, CKV), bf16),
            pltpu.VMEM((rep, group, 8, query_count), f32),
            pltpu.VMEM((dp, group, share_rows, CKV), bf16),
            pltpu.VMEM((dp, group, share_rows, 128), f32),
            pltpu.VMEM((dp, group, share_rows, CKV), bf16),
            pltpu.VMEM((dp, group, share_rows, 128), f32),
            pltpu.VMEM((rep, group, rows_here, inner), bf16),
            pltpu.VMEM(up_value.shape, bf16),
            pltpu.VMEM(out_proj.shape, bf16),
            pltpu.VMEM(w_gate.shape, bf16),
            pltpu.VMEM(w_up.shape, bf16),
            pltpu.VMEM(w_down.shape, bf16),
            pltpu.VMEM((rows, inner), bf16),
            pltpu.VMEM((dp, rows_here, width), bf16),
            pltpu.VMEM((dp, rows, width), bf16),
            pltpu.VMEM((dp, rows_here, width), f32),
            pltpu.VMEM((rows, width), bf16),
            pltpu.VMEM((rep, rows, 128), f32),
            pltpu.VMEM((rep, chunks, 2, rows, hidden_width // chunks), bf16),
            pltpu.VMEM((rows, hidden_width), bf16),
            pltpu.VMEM((dp, rows_here, width), bf16),
            pltpu.VMEM((dp, rows_here, width), bf16),
            dma((6,)),
            dma((dp - 1,)),
            dma((dp - 1,)),
            dma((dp - 1, rep - 1)),
            dma((dp - 1, rep - 1)),
            dma((2, rep - 1)),
            dma((2, rep - 1)),
            dma((2, dp - 1)),
            dma((2, dp - 1)),
            dma((rep - 1,)),
            dma((rep - 1,)),
            dma((dp - 1,)),
            dma((dp - 1,)),
            dma((dp - 1,)),
            dma((dp - 1,)),
            dma((rep - 1,)),
            dma((rep - 1,)),
            dma((chunks, rep - 1)),
            dma((chunks, rep - 1)),
            dma((dp - 1,)),
            dma((dp - 1,)),
        ],
        compiler_params=pltpu.CompilerParams(
            collective_id=0, has_side_effects=True, vmem_limit_bytes=60 * 1024 * 1024
        ),
    )(
        query_rows,
        fresh_page,
        bias,
        residual,
        norm_gain.reshape(1, -1),
        latent_store,
        up_value,
        out_proj,
        w_gate,
        w_up,
        w_down,
    )


def on_device(
    latent_store,
    page_rank,
    page_index,
    lengths,
    queries,
    new_latent,
    up_value,
    out_proj,
    residual,
    norm_gain,
    w_gate,
    w_up,
    w_down,
):
    my_rank = lax.axis_index("dp")
    my_column = lax.axis_index("rep")
    rep = lax.axis_size("rep")
    rank_count, slot_count = page_rank.shape
    page_count = latent_store.shape[1]
    requests = lengths.shape[1]
    rows_here = residual.shape[0]
    steps_count = rows_here // requests
    latent_width = new_latent.shape[1]
    head_count = queries.shape[1] // latent_width
    query_rows = queries.reshape(rows_here, head_count, latent_width).transpose(1, 0, 2)
    query_rows = query_rows.reshape(rep, head_count * rows_here // rep, latent_width)
    fresh_page = jnp.pad(new_latent.T, ((0, 0), (0, PAGE - rows_here)))
    global_slot = my_column * slot_count + jnp.arange(slot_count, dtype=jnp.int32)
    row_ids = jnp.arange(rows_here, dtype=jnp.int32)
    row_request = row_ids // steps_count
    slot_counts = jnp.where(
        (global_slot // PAGES)[None, None, :] == row_request[None, :, None],
        jnp.clip(
            jnp.repeat(lengths, steps_count, axis=1)[:, :, None]
            - (global_slot % PAGES * PAGE)[None, None, :],
            0,
            PAGE,
        ),
        0,
    )
    named = (page_rank == my_rank)[:, :, None] & (
        page_index[:, :, None] == jnp.arange(page_count, dtype=jnp.int32)
    )
    limits = jnp.sum(jnp.where(named[:, None], slot_counts[..., None], 0), axis=2)
    places = jnp.arange(PAGE, dtype=jnp.int32)
    seen = places < limits[..., None]
    fresh_seen = (places[None, :] <= row_ids[:, None]) & (
        places[None, :] // steps_count == row_request[:, None]
    )
    fresh_seen = (
        fresh_seen[None]
        & (jnp.arange(rank_count) == my_rank)[:, None, None]
        & (my_column == 0)
    )
    bias = jnp.concatenate([seen, fresh_seen[:, :, None]], axis=2).astype(jnp.float32)
    bias = bias.reshape(rank_count, rows_here, -1)
    return layer(
        query_rows,
        fresh_page,
        bias,
        residual,
        norm_gain,
        latent_store,
        up_value,
        out_proj,
        w_gate,
        w_up,
        w_down,
    )


def solution(mesh):
    in_specs = (
        P(("groups", "dp"), "rep", None, None),
        P("groups", "rep"),
        P("groups", "rep"),
        P("groups", None),
        P(("groups", "dp"), None),
        P(("groups", "dp"), None),
        P("dp", None, None),
        P("dp", "rep"),
        P(("groups", "dp"), "rep"),
        P("rep"),
        P("rep", "dp"),
        P("rep", "dp"),
        P("dp", "rep"),
    )
    out_specs = P(("groups", "dp"), "rep")
    return jax.shard_map(
        on_device, mesh=mesh, in_specs=in_specs, out_specs=out_specs, check_vma=False
    )
```

profile of v0, /device:TPU:0, one launch (start us, length us, event | category | flops | bytes accessed | tf_op | source)
XLA Modules:
  0.0 67.9 jit_solution(11452172226828347452)
XLA Ops:
  0.0 1.1 %reshape.188 = bf16[2,64,576]{2,1,0:T(8,128)(2,1)S(1)} reshape(bf16[2,36864]{1,0:T(2,128)(2,1)} %param.17) | data formatting | bytes 294912 | tf_op jit(solution)/shard_map/reshape | solution.py:499
  1.1 0.2 copy.24
  1.3 0.8 %reshape.189.query_ref = bf16[4,32,576]{2,1,0:T(8,128)(2,1)} reshape(bf16[64,2,576]{2,1,0:T(2,128)(2,1)S(1)} %bitcast.5) | data formatting | bytes 294912 | tf_op jit(solution)/shard_map/reshape | solution.py:500
  2.1 0.9 %copy.19 = bf16[2,576]{0,1:T(8,128)(2,1)S(1)} copy(bf16[2,576]{1,0:T(2,128)(2,1)} %param.18) | data formatting | bytes 4608 | tf_op args[5]
  2.9 0.7 %pad.4.fresh_ref = bf16[576,128]{1,0:T(8,128)(2,1)} pad(bf16[576,2]{1,0:T(8,128)(2,1)S(1)} %bitcast.6, bf16[]{:T(256)} %constant.52.clone.1), padding=0_0x0_126 | pad | bytes 149762 | tf_op jit(solution)/shard_map/jit(_pad)/pad | solution.py:501
  3.6 0.1 compare_and_fusion
  3.7 0.1 and_and_fusion
  3.8 0.1 broadcast_compare_fusion.1
  3.9 0.7 %clamp_select_fusion = s32[4,2,12]{0,2,1:T(8,128)S(1)} fusion(s32[12]{0:T(128)S(1)} %get-tuple-element.6, s32[4]{0:T(128)} %bitcast.7, pred[2,12]{1,0:T(4,128)(4,1)S(1)} %broadcast_compare_fusion.1), kind=kLoop, calls=%fused_computation.6 | loop fusion | flops 288 | bytes 472 | tf_op jit(solution)/shard_map/jit(_where)/select_n | solution.py:505
  4.6 0.8 %copy.21 = s32[4,12]{0,1:T(8,128)S(1)} copy(s32[4,12]{1,0:T(4,128)} %param.15) | data formatting | bytes 384 | tf_op args[2]
  5.4 0.7 %broadcast_compare_fusion = pred[4,12]{1,0:T(4,128)(4,1)S(1)} fusion(s32[4,12]{1,0:T(4,128)} %param.14, s32[]{:T(128)S(6)} %axis_index.23), kind=kLoop, calls=%fused_computation.19 | loop fusion | flops 48 | bytes 244 | tf_op jit(solution)/shard_map/eq | solution.py:515
  6.1 0.1 copy.20
  6.2 0.1 fusion
  6.3 0.1 select_reduce_fusion
  6.4 0.1 iota_compare_fusion
  6.5 0.7 reshape.191.bias_ref
  7.2 1.3 %reshape.190.gain_ref = f32[1,1792]{1,0:T(1,128)} reshape(f32[1792]{0:T(1024)} %param.22) | data formatting | bytes 14336 | tf_op jit(solution)/shard_map/reshape | solution.py:464
  8.4 58.2 %shard_map.130 = bf16[2,1792]{1,0:T(2,128)(2,1)} custom-call(bf16[4,32,576]{2,1,0:T(8,128)(2,1)} %reshape.189.query_ref, bf16[576,128]{1,0:T(8,128)(2,1)} %pad.4.fresh_ref, f32[4,2,1664]{2,1,0:T(2,128)} %reshape.191.bias_ref, bf16[2,1792]{1,0:T(2,128)(2,1)} %residual_ref.1, f32[1,1792]{1,0:T(1,128)} %reshape.190.gain_ref, ...), custom_call_target="tpu_custom_call" | custom-call | tf_op jit(solution)/shard_map/pallas_call | solution.py:401
  66.7 1.3 %copy.26 = bf16[2,1792]{1,0:T(2,128)(2,1)} copy(bf16[2,1792]{1,0:T(2,128)(2,1)} %shard_map.130) | data formatting | bytes 14336
  (6 shorter events, 0.0 us)
where the time goes:
time: 68.3 us; the launch traced here: 67.9 us
  Pallas kernels  58.2 us (85%)
  local copies, waits for them, and re-layouts  7.74 us (11%)
  other arithmetic  1.96 us (3%)
    pallas_call x1, Pallas kernels, layer(): pl.pallas_call(functools.partial(layer_kernel, dp, rep), out_shape=jax.Sh...  58.2 us
    unnamed x3, local copies, waits for them, and re-layouts  2.93 us

commit v1 on v0

v1 whole, which is shorter than its diff:
```python
import functools
import math

import jax
import jax.numpy as jnp
from jax import lax
from jax.experimental import pallas as pl
from jax.experimental.pallas import tpu as pltpu
from jax.sharding import PartitionSpec as P

D = 7168
CKV = 512
PAGE = 128
CORES = 2

score_scale = 1.0 / math.sqrt(192.0)
epsilon = 1e-06
mask_value = -1e30
tiny = 1e-30

MESH = pl.DeviceIdType.MESH
f32, bf16, i32 = jnp.float32, jnp.bfloat16, jnp.int32


def split_three(value):
    first = value.astype(bf16)
    rest = value - first.astype(f32)
    second = rest.astype(bf16)
    third = (rest - second.astype(f32)).astype(bf16)
    return first, second, third


def layer_kernel(
    dp,
    rep,
    page_rank,
    page_index,
    lengths,
    queries_hbm,
    fresh_hbm,
    residual_hbm,
    gain_hbm,
    store_hbm,
    up_value_hbm,
    out_proj_hbm,
    w_gate_hbm,
    w_up_hbm,
    w_down_hbm,
    out_ref,
    query_raw,
    fresh_raw,
    residual,
    gain,
    pages,
    up_value,
    out_proj,
    w_gate,
    w_up,
    w_down,
    queries,
    own_pages,
    peer_pages,
    own_limits,
    peer_limits,
    part,
    part_recv,
    latent,
    value_buf,
    level_buf,
    op_buf,
    mixed,
    sq_buf,
    gu_buf,
    down_send,
    down_recv,
    load_sem,
    q_send,
    q_recv,
    pg_send,
    pg_recv,
    lm_send,
    lm_recv,
    p_send,
    p_recv,
    v_send,
    v_recv,
    op_send,
    op_recv,
    sq_send,
    sq_recv,
    gu_send,
    gu_recv,
    dn_send,
    dn_recv,
):
    my_rank = lax.axis_index("dp")
    my_column = lax.axis_index("rep")
    my_core = lax.rem(my_column, CORES)
    my_plane = my_column // CORES
    steps, width = residual.shape
    rows = dp * steps
    latent_width = fresh_raw.shape[1]
    slots = page_rank.shape[1]
    slot_total = slots * rep
    half = up_value.shape[0]
    head_group = half * CORES
    block = half * steps
    query_count = dp * block
    cap = own_pages.shape[1]
    vdim = up_value.shape[2]

    barrier = pltpu.get_barrier_semaphore()
    columns = [lax.rem(my_column + k, rep) for k in range(1, rep)]
    low = 1 - my_rank // (dp // 2)
    near = low * my_rank + (1 - low) * (dp - 1 - my_rank)

    def mirror(d):
        return low * d + (1 - low) * (dp - 1 - d)

    def at_least(a, b):
        return (a - b + dp) // dp

    def far_peer(j):
        p = dp - 1 - j
        return mirror(p - at_least(near, p))

    def source(i):
        j = i - 1
        other = j - dp // 2
        late = at_least(j, dp // 2)
        return mirror((1 - late) * (dp // 2 + j) + late * (other + at_least(other, near)))

    ranks = [far_peer(j) for j in range(dp - 1)]
    for peer in ranks:
        pl.semaphore_signal(barrier, inc=1, device_id={"dp": peer}, device_id_type=MESH)
    for peer in columns:
        pl.semaphore_signal(barrier, inc=1, device_id={"rep": peer}, device_id_type=MESH)

    loads = []
    for i, (start, target) in enumerate(
        (
            (queries_hbm, query_raw),
            (store_hbm.at[0], pages),
            (fresh_hbm, fresh_raw),
            (residual_hbm, residual),
            (gain_hbm, gain),
            (up_value_hbm.at[pl.ds(my_core * half, half)], up_value),
            (out_proj_hbm, out_proj),
            (w_gate_hbm, w_gate),
            (w_up_hbm, w_up),
            (w_down_hbm, w_down),
        )
    ):
        copy = pltpu.make_async_copy(start, target, load_sem.at[i])
        copy.start()
        loads.append(copy)

    def to(target, start, end, send, recv):
        return pltpu.make_async_remote_copy(
            src_ref=start,
            dst_ref=end,
            send_sem=send,
            recv_sem=recv,
            device_id=target,
            device_id_type=MESH,
        )

    def spread(start, end, send, recv):
        copies = [
            to({"rep": peer}, start, end, send.at[k], recv.at[k])
            for k, peer in enumerate(columns)
        ]
        for copy in copies:
            copy.start()
        return copies

    loads[0].wait()
    pieces = []
    for p in range(dp):
        if half * latent_width % 128 == 0:
            at = pl.ds(
                pl.multiple_of((p * head_group + my_core * half) * latent_width, 128),
                half * latent_width,
            )
            chunk = query_raw[:, at].astype(f32)
        else:
            both = query_raw[
                :, p * head_group * latent_width : (p + 1) * head_group * latent_width
            ].astype(f32)
            chunk = jnp.where(
                my_core == 0, both[:, : half * latent_width], both[:, half * latent_width :]
            )
        for s in range(steps):
            for h in range(half):
                pieces.append(chunk[s : s + 1, h * latent_width : (h + 1) * latent_width])
    for r in range(0, query_count, 16):
        queries[my_rank, r : r + 16] = jnp.concatenate(pieces[r : r + 16], axis=0).astype(bf16)

    pl.semaphore_wait(barrier, dp - 1 + rep - 1)

    q_copies = []
    for j, peer in enumerate(ranks):
        copy = to(
            {"dp": peer},
            queries.at[my_rank],
            queries.at[my_rank],
            q_send.at[j],
            q_recv.at[my_rank],
        )
        copy.start()
        q_copies.append(copy)

    partner = my_plane * CORES + (1 - my_core)
    limit_rows = lax.broadcasted_iota(i32, own_limits.shape[1:], 0)
    loads[1].wait()

    def compact(i, carry):
        d = my_rank if isinstance(i, int) and i == 0 else source(i)
        count = jnp.int32(0)
        index = [jnp.int32(0)] * cap
        limit = [jnp.int32(0)] * cap
        for q in range(slots):
            held = jnp.where(page_rank[d, q] == my_rank, 1, 0)
            place = lax.rem(my_column * slots + q, slot_total) * PAGE
            seen = jnp.clip(lengths[d, 0] - place, 0, PAGE)
            for j in range(cap):
                hit = jnp.where(count == j, held, 0)
                index[j] = index[j] + hit * page_index[d, q]
                limit[j] = limit[j] + hit * seen
            count = count + held
        levels = jnp.zeros(limit_rows.shape, i32)
        for j in range(cap):
            own_pages[d, j] = pages[index[j]]
            levels = jnp.where(limit_rows == j, limit[j], levels)
        own_limits[d] = levels
        to({"rep": partner}, own_pages.at[d], peer_pages.at[d], pg_send.at[d], pg_recv.at[d]).start()
        to(
            {"rep": partner}, own_limits.at[d], peer_limits.at[d], lm_send.at[d], lm_recv.at[d]
        ).start()
        return carry

    compact(0, 0)
    if dp <= 4:
        for i in range(1, dp):
            compact(i, 0)
    else:
        lax.fori_loop(1, dp, compact, 0)

    lanes = lax.broadcasted_iota(i32, (query_count, PAGE), 1)
    row_ids = lax.broadcasted_iota(i32, (query_count, PAGE), 0)

    def attend(i, carry):
        first = isinstance(i, int) and i == 0
        if first:
            d = my_rank
        else:
            d = source(i)
            to({"dp": d}, queries.at[d], queries.at[d], q_send.at[0], q_recv.at[d]).wait_recv()
        to(
            {"rep": partner}, own_pages.at[d], peer_pages.at[d], pg_send.at[d], pg_recv.at[d]
        ).wait_recv()
        to(
            {"rep": partner}, own_limits.at[d], peer_limits.at[d], lm_send.at[d], lm_recv.at[d]
        ).wait_recv()
        query = queries[d]
        keys, visible = [], []
        for pages_ref, limits_ref in ((own_pages, own_limits), (peer_pages, peer_limits)):
            for j in range(cap):
                keys.append(pages_ref[d, j])
                visible.append(lanes < limits_ref[d, j : j + 1, :])
        keys = jnp.concatenate(keys, axis=1)
        score = jnp.dot(query, keys, preferred_element_type=f32) * score_scale
        scores = [
            jnp.where(see, score[:, n * PAGE : (n + 1) * PAGE], mask_value)
            for n, see in enumerate(visible)
        ]
        if first:
            loads[2].wait()
            fresh = jnp.concatenate(
                [fresh_raw[...].astype(f32), jnp.zeros((PAGE - steps, latent_width), f32)], axis=0
            ).astype(bf16)
            extra = lax.dot_general(
                query, fresh, (((1,), (1,)), ((), ())), preferred_element_type=f32
            )
            step = lax.rem(row_ids, block) // half
            see = lanes + PAGE * my_plane <= step
            visible.append(see)
            scores.append(jnp.where(see, extra * score_scale, mask_value))
        peak = jnp.max(functools.reduce(jnp.maximum, scores), axis=1, keepdims=True)
        weights = [
            jnp.where(see, jnp.exp(score - peak), 0.0)
            for see, score in zip(visible, scores, strict=True)
        ]
        total = jnp.sum(functools.reduce(jnp.add, weights), axis=1, keepdims=True)
        rounded = [weight.astype(bf16) for weight in weights]
        value = lax.dot_general(
            jnp.concatenate(rounded[: CORES * cap], axis=1),
            keys[:CKV],
            (((1,), (1,)), ((), ())),
            preferred_element_type=f32,
        )
        if first:
            value += jnp.dot(rounded[-1], fresh[:, :CKV], preferred_element_type=f32)
        value = value / jnp.maximum(total, tiny)
        level = jnp.where(total > 0.0, peak + jnp.log(jnp.maximum(total, tiny)), mask_value)
        one, two, three = (term.astype(f32) for term in split_three(level))
        stat = jnp.where(lanes == 0, one, jnp.where(lanes == 1, two, three))
        for p in range(dp):
            part[i, p, :, :CKV] = value[p * block : (p + 1) * block].astype(bf16)
            part[i, p, :, CKV:] = stat[p * block : (p + 1) * block].astype(bf16)
        for peer in ranks:
            to(
                {"dp": peer},
                part.at[i, peer],
                part_recv.at[d, my_rank],
                p_send.at[i],
                p_recv.at[d],
            ).start()
        part_recv[d, my_rank] = part[i, my_rank]
        return carry

    attend(0, 0)
    if dp <= 4:
        for i in range(1, dp):
            attend(i, 0)
    else:
        lax.fori_loop(1, dp, attend, 0)

    levels = []
    for d in range(dp):
        to(
            {"dp": ranks[0]},
            part.at[0, pl.ds(0, dp - 1)],
            part_recv.at[d, pl.ds(0, dp - 1)],
            p_send.at[0],
            p_recv.at[d],
        ).wait_recv()
        message = part_recv[d].astype(f32)
        level = (
            message[:, :, CKV : CKV + 1]
            + message[:, :, CKV + 1 : CKV + 2]
            + message[:, :, CKV + 2 : CKV + 3]
        )
        best = jnp.max(level, axis=0)
        factor = jnp.exp(level - best[None])
        total = jnp.sum(factor, axis=0)
        latent[d * block : (d + 1) * block] = (
            jnp.sum(message[:, :, :CKV] * factor, axis=0) / total
        )
        levels.append(best + jnp.log(total))
    loads[5].wait()
    projected = jnp.dot(
        latent[...].astype(bf16),
        jnp.concatenate([up_value[h] for h in range(half)], axis=1),
        preferred_element_type=f32,
    )
    row_head = lax.rem(lax.broadcasted_iota(i32, (query_count, 128), 0), half)
    level = jnp.where(
        row_head == lax.broadcasted_iota(i32, (query_count, 128), 1),
        jnp.concatenate(levels, axis=0),
        0.0,
    )
    picked = jnp.concatenate(
        [
            jnp.where(row_head[:, :vdim] == h, projected[:, h * vdim : (h + 1) * vdim], 0.0)
            for h in range(half)
        ],
        axis=1,
    )
    if half > 1:
        picked = jnp.sum(picked.reshape(rows, half, half * vdim), axis=1)
        level = jnp.sum(level.reshape(rows, half, 128), axis=1)
    value_buf[my_column] = picked.astype(bf16)
    level_buf[my_column] = level
    v_copies = spread(value_buf.at[my_column], value_buf.at[my_column], v_send.at[0], v_recv.at[0])
    v_copies += spread(level_buf.at[my_column], level_buf.at[my_column], v_send.at[1], v_recv.at[1])
    for copy in v_copies:
        copy.wait()
    values = []
    for k in range(CORES):
        held = range(k, rep, CORES)
        best = functools.reduce(jnp.maximum, [level_buf[c] for c in held])
        factors = [jnp.exp(level_buf[c] - best) for c in held]
        total = functools.reduce(jnp.add, factors)
        factors = [factor / total for factor in factors]
        for h in range(half):
            values.append(
                functools.reduce(
                    jnp.add,
                    [
                        value_buf[c, :, h * vdim : (h + 1) * vdim].astype(f32)
                        * factor[:, h : h + 1]
                        for c, factor in zip(held, factors, strict=True)
                    ],
                )
            )
    values = jnp.concatenate(values, axis=1).astype(bf16)

    loads[3].wait()
    loads[6].wait()
    own_row = lax.broadcasted_iota(i32, (rows, width), 0) // steps == my_rank
    whole = jnp.where(
        own_row, jnp.concatenate([residual[...].astype(f32)] * dp, axis=0), 0.0
    ) + jnp.dot(values, out_proj[...], preferred_element_type=f32)
    op_buf[my_rank] = whole.astype(bf16)
    op_copies = []
    for j, peer in enumerate(ranks):
        item = op_buf.at[my_rank]
        copy = to({"dp": peer}, item, item, op_send.at[j], op_recv.at[my_rank])
        copy.start()
        op_copies.append(copy)
    for peer in ranks:
        item = op_buf.at[peer]
        to({"dp": peer}, item, item, op_send.at[0], op_recv.at[peer]).wait_recv()
        whole += op_buf[peer].astype(f32)
    for d in range(dp):
        mixed[d] = whole[d * steps : (d + 1) * steps]
    sq_buf[my_column] = jnp.broadcast_to(
        jnp.sum(whole * whole, axis=1, keepdims=True), (rows, 128)
    )
    sq_copies = spread(sq_buf.at[my_column], sq_buf.at[my_column], sq_send, sq_recv)
    loads[4].wait()
    scaled = (whole * gain[...].reshape(1, width)).astype(bf16)

    chunks, chunk = gu_buf.shape[1], gu_buf.shape[4]
    loads[7].wait()
    loads[8].wait()
    gu_copies = []
    for c in range(chunks):
        at = slice(c * chunk, (c + 1) * chunk)
        gu_buf[my_column, c, 0] = jnp.dot(
            scaled, w_gate[:, at], preferred_element_type=f32
        ).astype(bf16)
        gu_buf[my_column, c, 1] = jnp.dot(
            scaled, w_up[:, at], preferred_element_type=f32
        ).astype(bf16)
        item = gu_buf.at[my_column, c]
        gu_copies.append(spread(item, item, gu_send.at[c], gu_recv.at[c]))

    for copy in sq_copies:
        copy.wait()
    total = sq_buf[0]
    for c in range(1, rep):
        total += sq_buf[c]
    scale = lax.rsqrt(total[:, :1] / D + epsilon)
    loads[9].wait()
    down = jnp.zeros((rows, width), f32)
    for c in range(chunks):
        for copy in gu_copies[c]:
            copy.wait()
        gate = gu_buf[0, c, 0].astype(f32)
        up = gu_buf[0, c, 1].astype(f32)
        for other in range(1, rep):
            gate += gu_buf[other, c, 0].astype(f32)
            up += gu_buf[other, c, 1].astype(f32)
        gate = gate * scale
        up = up * scale
        hidden = (gate / (1.0 + jnp.exp(-gate)) * up).astype(bf16)
        down += jnp.dot(
            hidden, w_down[c * chunk : (c + 1) * chunk], preferred_element_type=f32
        )
    for d in range(dp):
        down_send[d] = down[d * steps : (d + 1) * steps].astype(bf16)
    dn_copies = [
        to(
            {"dp": peer},
            down_send.at[peer],
            down_recv.at[my_rank],
            dn_send.at[k],
            dn_recv.at[my_rank],
        )
        for k, peer in enumerate(ranks)
    ]
    for copy in dn_copies:
        copy.start()
    result = mixed[my_rank] + down_send[my_rank].astype(f32)

    for copy in q_copies + op_copies:
        copy.wait_send()
    for d in range(dp):
        to({"rep": partner}, own_pages.at[d], peer_pages.at[d], pg_send.at[d], pg_recv.at[d]).wait_send()
        to(
            {"rep": partner}, own_limits.at[d], peer_limits.at[d], lm_send.at[d], lm_recv.at[d]
        ).wait_send()
        to(
            {"dp": ranks[0]},
            part.at[d, pl.ds(0, dp - 1)],
            part_recv.at[0, pl.ds(0, dp - 1)],
            p_send.at[d],
            p_recv.at[0],
        ).wait_send()

    for peer in ranks:
        to(
            {"dp": peer}, down_send.at[peer], down_recv.at[peer], dn_send.at[0], dn_recv.at[peer]
        ).wait_recv()
        result += down_recv[peer].astype(f32)
    for copy in dn_copies:
        copy.wait_send()
    out_ref[...] = result.astype(bf16)


def layer(
    latent_store,
    page_rank,
    page_index,
    lengths,
    queries,
    new_latent,
    up_value,
    out_proj,
    residual,
    norm_gain,
    w_gate,
    w_up,
    w_down,
):
    dp, rep = lax.axis_size("dp"), lax.axis_size("rep")
    steps, width = residual.shape
    rows = dp * steps
    hidden_width = w_gate.shape[1]
    latent_width = new_latent.shape[1]
    slots = latent_store.shape[1]
    cap = -(-slots // dp)
    half = up_value.shape[0] // CORES
    block = half * steps
    query_count = dp * block
    vdim = up_value.shape[2]
    chunks = 3 if hidden_width % (3 * 128) == 0 else 1
    dma = pltpu.SemaphoreType.DMA
    smem = pl.BlockSpec(memory_space=pltpu.SMEM)
    hbm = pl.BlockSpec(memory_space=pl.ANY)
    return pl.pallas_call(
        functools.partial(layer_kernel, dp, rep),
        out_shape=jax.ShapeDtypeStruct((steps, width), bf16),
        in_specs=[smem] * 3 + [hbm] * 10,
        out_specs=pl.BlockSpec(memory_space=pltpu.VMEM),
        scratch_shapes=[
            pltpu.VMEM(queries.shape, bf16),
            pltpu.VMEM(new_latent.shape, bf16),
            pltpu.VMEM(residual.shape, bf16),
            pltpu.VMEM(norm_gain.shape, f32),
            pltpu.VMEM(latent_store.shape[1:], bf16),
            pltpu.VMEM((half,) + up_value.shape[1:], bf16),
            pltpu.VMEM(out_proj.shape, bf16),
            pltpu.VMEM(w_gate.shape, bf16),
            pltpu.VMEM(w_up.shape, bf16),
            pltpu.VMEM(w_down.shape, bf16),
            pltpu.VMEM((dp, query_count, latent_width), bf16),
            pltpu.VMEM((dp, cap) + latent_store.shape[2:], bf16),
            pltpu.VMEM((dp, cap) + latent_store.shape[2:], bf16),
            pltpu.VMEM((dp, 8, PAGE), i32),
            pltpu.VMEM((dp, 8, PAGE), i32),
            pltpu.VMEM((dp, dp, block, CKV + PAGE), bf16),
            pltpu.VMEM((dp, dp, block, CKV + PAGE), bf16),
            pltpu.VMEM((query_count, CKV), f32),
            pltpu.VMEM((rep, rows, half * vdim), bf16),
            pltpu.VMEM((rep, rows, 128), f32),
            pltpu.VMEM((dp, rows, width), bf16),
            pltpu.VMEM((dp, steps, width), f32),
            pltpu.VMEM((rep, rows, 128), f32),
            pltpu.VMEM((rep, chunks, 2, rows, hidden_width // chunks), bf16),
            pltpu.VMEM((dp, steps, width), bf16),
            pltpu.VMEM((dp, steps, width), bf16),
            dma((10,)),
            dma((dp - 1,)),
            dma((dp,)),
            dma((dp,)),
            dma((dp,)),
            dma((dp,)),
            dma((dp,)),
            dma((dp,)),
            dma((dp,)),
            dma((2, rep - 1)),
            dma((2, rep - 1)),
            dma((dp - 1,)),
            dma((dp,)),
            dma((rep - 1,)),
            dma((rep - 1,)),
            dma((chunks, rep - 1)),
            dma((chunks, rep - 1)),
            dma((dp - 1,)),
            dma((dp,)),
        ],
        compiler_params=pltpu.CompilerParams(
            collective_id=0, has_side_effects=True, vmem_limit_bytes=60 * 1024 * 1024
        ),
    )(
        page_rank,
        page_index,
        lengths,
        queries,
        new_latent,
        residual,
        norm_gain,
        latent_store,
        up_value,
        out_proj,
        w_gate,
        w_up,
        w_down,
    )


def solution(mesh):
    in_specs = (
        P(("groups", "dp"), "rep", None, None),
        P("groups", "rep"),
        P("groups", "rep"),
        P("groups", None),
        P(("groups", "dp"), None),
        P(("groups", "dp"), None),
        P("dp", None, None),
        P("dp", "rep"),
        P(("groups", "dp"), "rep"),
        P("rep"),
        P("rep", "dp"),
        P("rep", "dp"),
        P("dp", "rep"),
    )
    out_specs = P(("groups", "dp"), "rep")
    return jax.shard_map(
        layer, mesh=mesh, in_specs=in_specs, out_specs=out_specs, check_vma=False
    )
```

time: 68.3 us -> 46.3 us (0.68)
  Pallas kernels: 58.2 us -> 43.4 us
  local copies, waits for them, and re-layouts: 7.74 us -> 2.61 us
  other arithmetic: 1.96 us -> 0 us
    pallas_call x1, Pallas kernels: 58.2 us -> 43.4 us  [layer(): pl.pallas_call(functools.partial(layer_kernel, dp, rep), out_shape=jax.Sh...]
    reshape x4 -> x0, local copies, waits for them, and re-layouts: 3.35 us -> none  [the longest x1 1.29 us: layer(): norm_gain.reshape(1, -1)]
    eq x3 -> x0, other arithmetic: 0.77 us -> none  [the longest x1 0.69 us: on_device(): page_rank == my_rank]
    select_n x4 -> x0, other arithmetic: 0.75 us -> none  [the longest x1 0.73 us: on_device(): jnp.where((global_slot // PAGES)[None, None, :] == row_request[None, :, N...]
    pad x1 -> x0, local copies, waits for them, and re-layouts: 0.68 us -> none  [on_device(): fresh_page = jnp.pad(new_latent.T, ((0, 0), (0, PAGE - rows_here)))]
    unnamed x3 -> x2, local copies, waits for them, and re-layouts: 2.93 us -> 2.61 us
where the time goes in v1:
time: 46.3 us; the launch traced here: 46.1 us
  Pallas kernels  43.4 us (94%)
  local copies, waits for them, and re-layouts  2.61 us (6%)
    pallas_call x1, Pallas kernels, layer(): pl.pallas_call(functools.partial(layer_kernel, dp, rep), out_shape=jax.Sh...  43.4 us
    unnamed x2, local copies, waits for them, and re-layouts  2.61 us

profile of v1, /device:TPU:0, one launch (start us, length us, event | category | flops | bytes accessed | tf_op | source)
XLA Modules:
  0.0 46.1 jit_solution(9918765263163550155)
XLA Ops:
  0.0 1.3 %copy.14.lengths = s32[4,1]{1,0:T(4,128)} copy(s32[4,1]{0,1:T(1,128)} %param.16) | data formatting | bytes 32 | tf_op args[3]
  1.3 43.4 %shard_map.127 = bf16[2,1792]{1,0:T(2,128)(2,1)} custom-call(s32[4,12]{1,0:T(4,128)} %page_rank.1, s32[4,12]{1,0:T(4,128)} %page_index.1, s32[4,1]{1,0:T(4,128)} %copy.14.lengths, bf16[2,36864]{1,0:T(2,128)(2,1)} %queries_hbm.1, bf16[2,576]{1,0:T(2,128)(2,1)} %fresh_hbm.1, bf16[2,1792]{1,0:T(2,128)(2,1)} %residual_hbm.1, f32[1792]{0:T(1024)} %gain_hbm.1, ...), custom_call_target="tpu_custom_call" | custom-call | tf_op jit(solution)/shard_map/pallas_call | solution.py:533
  44.8 1.3 %copy.16 = bf16[2,1792]{1,0:T(2,128)(2,1)} copy(bf16[2,1792]{1,0:T(2,128)(2,1)} %shard_map.127) | data formatting | bytes 14336

commit v2 on v1

--- a/solution.py
+++ b/solution.py
@@ -58,6 +58,7 @@
     w_up,
     w_down,
     queries,
+    tails,
     own_pages,
     peer_pages,
     own_limits,
@@ -76,6 +77,8 @@
     load_sem,
     q_send,
     q_recv,
+    t_send,
+    t_recv,
     pg_send,
     pg_recv,
     lm_send,
@@ -111,26 +114,15 @@
 
     barrier = pltpu.get_barrier_semaphore()
     columns = [lax.rem(my_column + k, rep) for k in range(1, rep)]
-    low = 1 - my_rank // (dp // 2)
-    near = low * my_rank + (1 - low) * (dp - 1 - my_rank)
-
-    def mirror(d):
-        return low * d + (1 - low) * (dp - 1 - d)
-
-    def at_least(a, b):
-        return (a - b + dp) // dp
-
-    def far_peer(j):
-        p = dp - 1 - j
-        return mirror(p - at_least(near, p))
+    bits = dp.bit_length() - 1
+
+    def flipped(mask):
+        return sum((my_rank // 2**b + mask // 2**b) % 2 * 2**b for b in range(bits))
 
     def source(i):
-        j = i - 1
-        other = j - dp // 2
-        late = at_least(j, dp // 2)
-        return mirror((1 - late) * (dp // 2 + j) + late * (other + at_least(other, near)))
-
-    ranks = [far_peer(j) for j in range(dp - 1)]
+        return flipped((0, 1, 3, 2)[i] if dp == 4 else i)
+
+    ranks = [source(i) for i in range(1, dp)]
     for peer in ranks:
         pl.semaphore_signal(barrier, inc=1, device_id={"dp": peer}, device_id_type=MESH)
     for peer in columns:
@@ -193,36 +185,51 @@
         for s in range(steps):
             for h in range(half):
                 pieces.append(chunk[s : s + 1, h * latent_width : (h + 1) * latent_width])
+    tail_rows = []
     for r in range(0, query_count, 16):
-        queries[my_rank, r : r + 16] = jnp.concatenate(pieces[r : r + 16], axis=0).astype(bf16)
+        whole = jnp.concatenate(pieces[r : r + 16], axis=0)
+        queries[my_rank, r : r + 16] = whole[:, :CKV].astype(bf16)
+        tail_rows.append(whole[:, CKV:])
+    tail = jnp.concatenate(tail_rows, axis=0)
+    tails[my_rank] = jnp.concatenate(
+        [tail[: query_count // 2], tail[query_count // 2 :]], axis=1
+    ).astype(bf16)
 
     pl.semaphore_wait(barrier, dp - 1 + rep - 1)
+
+    def query_copies(peer, d, j):
+        return (
+            to({"dp": peer}, queries.at[d], queries.at[d], q_send.at[j], q_recv.at[d]),
+            to({"dp": peer}, tails.at[d], tails.at[d], t_send.at[j], t_recv.at[d]),
+        )
 
     q_copies = []
     for j, peer in enumerate(ranks):
-        copy = to(
-            {"dp": peer},
-            queries.at[my_rank],
-            queries.at[my_rank],
-            q_send.at[j],
-            q_recv.at[my_rank],
-        )
-        copy.start()
-        q_copies.append(copy)
+        for copy in query_copies(peer, my_rank, j):
+            copy.start()
+            q_copies.append(copy)
 
     partner = my_plane * CORES + (1 - my_core)
     limit_rows = lax.broadcasted_iota(i32, own_limits.shape[1:], 0)
     loads[1].wait()
 
+    def page_copies(d):
+        return (
+            to({"rep": partner}, own_pages.at[d], peer_pages.at[d], pg_send.at[d], pg_recv.at[d]),
+            to(
+                {"rep": partner}, own_limits.at[d], peer_limits.at[d], lm_send.at[d], lm_recv.at[d]
+            ),
+        )
+
     def compact(i, carry):
-        d = my_rank if isinstance(i, int) and i == 0 else source(i)
+        d = source(i)
         count = jnp.int32(0)
         index = [jnp.int32(0)] * cap
         limit = [jnp.int32(0)] * cap
         for q in range(slots):
             held = jnp.where(page_rank[d, q] == my_rank, 1, 0)
             place = lax.rem(my_column * slots + q, slot_total) * PAGE
-            seen = jnp.clip(lengths[d, 0] - place, 0, PAGE)
+            seen = jnp.clip(lengths[0, d] - place, 0, PAGE)
             for j in range(cap):
                 hit = jnp.where(count == j, held, 0)
                 index[j] = index[j] + hit * page_index[d, q]
@@ -233,10 +240,8 @@
             own_pages[d, j] = pages[index[j]]
             levels = jnp.where(limit_rows == j, limit[j], levels)
         own_limits[d] = levels
-        to({"rep": partner}, own_pages.at[d], peer_pages.at[d], pg_send.at[d], pg_recv.at[d]).start()
-        to(
-            {"rep": partner}, own_limits.at[d], peer_limits.at[d], lm_send.at[d], lm_recv.at[d]
-        ).start()
+        for copy in page_copies(d):
+            copy.start()
         return carry
 
     compact(0, 0)
@@ -249,27 +254,42 @@
     lanes = lax.broadcasted_iota(i32, (query_count, PAGE), 1)
     row_ids = lax.broadcasted_iota(i32, (query_count, PAGE), 0)
 
+    def send_part(i):
+        d = source(i)
+        for peer in ranks:
+            to(
+                {"dp": peer},
+                part.at[i, peer],
+                part_recv.at[d, my_rank],
+                p_send.at[i],
+                p_recv.at[d],
+            ).start()
+
     def attend(i, carry):
         first = isinstance(i, int) and i == 0
-        if first:
-            d = my_rank
-        else:
-            d = source(i)
-            to({"dp": d}, queries.at[d], queries.at[d], q_send.at[0], q_recv.at[d]).wait_recv()
-        to(
-            {"rep": partner}, own_pages.at[d], peer_pages.at[d], pg_send.at[d], pg_recv.at[d]
-        ).wait_recv()
-        to(
-            {"rep": partner}, own_limits.at[d], peer_limits.at[d], lm_send.at[d], lm_recv.at[d]
-        ).wait_recv()
+        d = source(i)
+        if not first:
+            for copy in query_copies(d, d, 0):
+                copy.wait_recv()
+        for copy in page_copies(d):
+            copy.wait_recv()
+        if not first and isinstance(i, int) and i == 1:
+            send_part(0)
         query = queries[d]
+        tail = tails[d].astype(f32)
+        tail = jnp.concatenate(
+            [tail[:, : latent_width - CKV], tail[:, latent_width - CKV :]], axis=0
+        ).astype(bf16)
         keys, visible = [], []
         for pages_ref, limits_ref in ((own_pages, own_limits), (peer_pages, peer_limits)):
             for j in range(cap):
                 keys.append(pages_ref[d, j])
                 visible.append(lanes < limits_ref[d, j : j + 1, :])
         keys = jnp.concatenate(keys, axis=1)
-        score = jnp.dot(query, keys, preferred_element_type=f32) * score_scale
+        score = (
+            jnp.dot(query, keys[:CKV], preferred_element_type=f32)
+            + jnp.dot(tail, keys[CKV:], preferred_element_type=f32)
+        ) * score_scale
         scores = [
             jnp.where(see, score[:, n * PAGE : (n + 1) * PAGE], mask_value)
             for n, see in enumerate(visible)
@@ -279,9 +299,10 @@
             fresh = jnp.concatenate(
                 [fresh_raw[...].astype(f32), jnp.zeros((PAGE - steps, latent_width), f32)], axis=0
             ).astype(bf16)
+            across = (((1,), (1,)), ((), ()))
             extra = lax.dot_general(
-                query, fresh, (((1,), (1,)), ((), ())), preferred_element_type=f32
-            )
+                query, fresh[:, :CKV], across, preferred_element_type=f32
+            ) + lax.dot_general(tail, fresh[:, CKV:], across, preferred_element_type=f32)
             step = lax.rem(row_ids, block) // half
             see = lanes + PAGE * my_plane <= step
             visible.append(see)
@@ -308,14 +329,8 @@
         for p in range(dp):
             part[i, p, :, :CKV] = value[p * block : (p + 1) * block].astype(bf16)
             part[i, p, :, CKV:] = stat[p * block : (p + 1) * block].astype(bf16)
-        for peer in ranks:
-            to(
-                {"dp": peer},
-                part.at[i, peer],
-                part_recv.at[d, my_rank],
-                p_send.at[i],
-                p_recv.at[d],
-            ).start()
+        if not first:
+            send_part(i)
         part_recv[d, my_rank] = part[i, my_rank]
         return carry
 
@@ -324,6 +339,7 @@
         for i in range(1, dp):
             attend(i, 0)
     else:
+        send_part(0)
         lax.fori_loop(1, dp, attend, 0)
 
     levels = []
@@ -335,6 +351,7 @@
             p_send.at[0],
             p_recv.at[d],
         ).wait_recv()
+    for d in range(dp):
         message = part_recv[d].astype(f32)
         level = (
             message[:, :, CKV : CKV + 1]
@@ -478,10 +495,8 @@
     for copy in q_copies + op_copies:
         copy.wait_send()
     for d in range(dp):
-        to({"rep": partner}, own_pages.at[d], peer_pages.at[d], pg_send.at[d], pg_recv.at[d]).wait_send()
-        to(
-            {"rep": partner}, own_limits.at[d], peer_limits.at[d], lm_send.at[d], lm_recv.at[d]
-        ).wait_send()
+        for copy in page_copies(d):
+            copy.wait_send()
         to(
             {"dp": ranks[0]},
             part.at[d, pl.ds(0, dp - 1)],
@@ -497,7 +512,7 @@
         result += down_recv[peer].astype(f32)
     for copy in dn_copies:
         copy.wait_send()
-    out_ref[...] = result.astype(bf16)
+    out_ref[...] = result
 
 
 def layer(
@@ -526,13 +541,13 @@
     block = half * steps
     query_count = dp * block
     vdim = up_value.shape[2]
-    chunks = 3 if hidden_width % (3 * 128) == 0 else 1
+    chunks = hidden_width // (512 if hidden_width % 512 == 0 else 128)
     dma = pltpu.SemaphoreType.DMA
     smem = pl.BlockSpec(memory_space=pltpu.SMEM)
     hbm = pl.BlockSpec(memory_space=pl.ANY)
     return pl.pallas_call(
         functools.partial(layer_kernel, dp, rep),
-        out_shape=jax.ShapeDtypeStruct((steps, width), bf16),
+        out_shape=jax.ShapeDtypeStruct((steps, width), f32),
         in_specs=[smem] * 3 + [hbm] * 10,
         out_specs=pl.BlockSpec(memory_space=pltpu.VMEM),
         scratch_shapes=[
@@ -546,7 +561,8 @@
             pltpu.VMEM(w_gate.shape, bf16),
             pltpu.VMEM(w_up.shape, bf16),
             pltpu.VMEM(w_down.shape, bf16),
-            pltpu.VMEM((dp, query_count, latent_width), bf16),
+            pltpu.VMEM((dp, query_count, CKV), bf16),
+            pltpu.VMEM((dp, query_count // 2, 2 * (latent_width - CKV)), bf16),
             pltpu.VMEM((dp, cap) + latent_store.shape[2:], bf16),
             pltpu.VMEM((dp, cap) + latent_store.shape[2:], bf16),
             pltpu.VMEM((dp, 8, PAGE), i32),
@@ -565,6 +581,8 @@
             dma((10,)),
             dma((dp - 1,)),
             dma((dp,)),
+            dma((dp - 1,)),
+            dma((dp,)),
             dma((dp,)),
             dma((dp,)),
             dma((dp,)),
@@ -588,7 +606,7 @@
     )(
         page_rank,
         page_index,
-        lengths,
+        lengths.T,
         queries,
         new_latent,
         residual,
@@ -599,7 +617,7 @@
         w_gate,
         w_up,
         w_down,
-    )
+    ).astype(bf16)
 
 
 def solution(mesh):

time: 46.3 us -> 44 us (0.950)
  local copies, waits for them, and re-layouts: 2.61 us -> 0 us
  other arithmetic: 0 us -> 1.31 us
  Pallas kernels: 43.4 us -> 42.5 us
    unnamed x2 -> x0, local copies, waits for them, and re-layouts: 2.61 us -> none
    convert_element_type x0 -> x1, other arithmetic: none -> 1.31 us  [layer(): return pl.pallas_call(functools.partial(layer_kernel, dp, rep), out_shape...]
    pallas_call x1, Pallas kernels: 43.4 us -> 42.5 us  [layer(): pl.pallas_call(functools.partial(layer_kernel, dp, rep), out_shape=jax.Sh...]
where the time goes in v2:
time: 44 us; the launch traced here: 43.8 us
  Pallas kernels  42.5 us (97%)
  other arithmetic  1.31 us (3%)
    pallas_call x1, Pallas kernels, layer(): pl.pallas_call(functools.partial(layer_kernel, dp, rep), out_shape=jax.Sh...  42.5 us
    convert_element_type x1, other arithmetic, layer(): return pl.pallas_call(functools.partial(layer_kernel, dp, rep), out_shape...  1.31 us

profile of v2, /device:TPU:0, one launch (start us, length us, event | category | flops | bytes accessed | tf_op | source)
XLA Modules:
  0.0 43.8 jit_solution(10565061849842166052)
XLA Ops:
  0.0 42.5 %shard_map.127 = f32[2,1792]{1,0:T(2,128)} custom-call(s32[4,12]{1,0:T(4,128)} %page_rank.1, s32[4,12]{1,0:T(4,128)} %page_index.1, s32[1,4]{1,0:T(1,128)} %bitcast.1, bf16[2,36864]{1,0:T(2,128)(2,1)} %queries_hbm.1, bf16[2,576]{1,0:T(2,128)(2,1)} %fresh_hbm.1, bf16[2,1792]{1,0:T(2,128)(2,1)} %residual_hbm.1, f32[1792]{0:T(1024)} %gain_hbm.1, ...), custom_call_target="tpu_custom_call" | custom-call | tf_op jit(solution)/shard_map/pallas_call | solution.py:548
  42.5 1.3 %convert_element_type.3 = bf16[2,1792]{1,0:T(2,128)(2,1)} convert(f32[2,1792]{1,0:T(2,128)} %shard_map.127) | non-fusion elementwise | flops 3584 | bytes 21504 | tf_op jit(solution)/shard_map/convert_element_type | solution.py:620

commit v3 on v2

--- a/solution.py
+++ b/solution.py
@@ -33,9 +33,9 @@
 def layer_kernel(
     dp,
     rep,
-    page_rank,
-    page_index,
-    lengths,
+    page_rank_hbm,
+    page_index_hbm,
+    lengths_hbm,
     queries_hbm,
     fresh_hbm,
     residual_hbm,
@@ -47,6 +47,9 @@
     w_up_hbm,
     w_down_hbm,
     out_ref,
+    page_rank,
+    page_index,
+    lengths,
     query_raw,
     fresh_raw,
     residual,
@@ -68,9 +71,11 @@
     latent,
     value_buf,
     level_buf,
-    op_buf,
+    op_first,
+    op_second,
     mixed,
     sq_buf,
+    gu_sum,
     gu_buf,
     down_send,
     down_recv,
@@ -79,6 +84,8 @@
     q_recv,
     t_send,
     t_recv,
+    x_send,
+    x_recv,
     pg_send,
     pg_recv,
     lm_send,
@@ -141,11 +148,14 @@
             (w_gate_hbm, w_gate),
             (w_up_hbm, w_up),
             (w_down_hbm, w_down),
+            (page_rank_hbm, page_rank),
+            (page_index_hbm, page_index),
+            (lengths_hbm, lengths),
         )
     ):
-        copy = pltpu.make_async_copy(start, target, load_sem.at[i])
-        copy.start()
-        loads.append(copy)
+        loads.append(pltpu.make_async_copy(start, target, load_sem.at[i]))
+    for i in (0, 10, 11, 12, *range(1, 10)):
+        loads[i].start()
 
     def to(target, start, end, send, recv):
         return pltpu.make_async_remote_copy(
@@ -185,23 +195,38 @@
         for s in range(steps):
             for h in range(half):
                 pieces.append(chunk[s : s + 1, h * latent_width : (h + 1) * latent_width])
-    tail_rows = []
-    for r in range(0, query_count, 16):
-        whole = jnp.concatenate(pieces[r : r + 16], axis=0)
-        queries[my_rank, r : r + 16] = whole[:, :CKV].astype(bf16)
-        tail_rows.append(whole[:, CKV:])
-    tail = jnp.concatenate(tail_rows, axis=0)
-    tails[my_rank] = jnp.concatenate(
-        [tail[: query_count // 2], tail[query_count // 2 :]], axis=1
-    ).astype(bf16)
+    planes, share = queries.shape[1:3]
+    for x in range(planes):
+        whole = jnp.concatenate(pieces[x * share : (x + 1) * share], axis=0)
+        queries[my_rank, x] = whole[:, :CKV].astype(bf16)
+        tails[my_rank, x] = jnp.concatenate(
+            [whole[: share // 2, CKV:], whole[share // 2 :, CKV:]], axis=1
+        ).astype(bf16)
 
     pl.semaphore_wait(barrier, dp - 1 + rep - 1)
 
     def query_copies(peer, d, j):
-        return (
-            to({"dp": peer}, queries.at[d], queries.at[d], q_send.at[j], q_recv.at[d]),
-            to({"dp": peer}, tails.at[d], tails.at[d], t_send.at[j], t_recv.at[d]),
-        )
+        return [
+            to({"dp": peer}, item.at[d, my_plane], item.at[d, my_plane], send.at[j], recv.at[d])
+            for item, send, recv in ((queries, q_send, q_recv), (tails, t_send, t_recv))
+        ]
+
+    def plane_copies(d, i, arriving):
+        copies = []
+        for j in range(1, planes):
+            peer = lax.rem(my_plane + j, planes) * CORES + my_core
+            x = lax.rem(my_plane + planes - j, planes) if arriving else my_plane
+            for n, item in enumerate((queries, tails)):
+                copies.append(
+                    to(
+                        {"rep": peer},
+                        item.at[d, x],
+                        item.at[d, x],
+                        x_send.at[n, i, j - 1],
+                        x_recv.at[n, d, j - 1],
+                    )
+                )
+        return copies
 
     q_copies = []
     for j, peer in enumerate(ranks):
@@ -211,7 +236,8 @@
 
     partner = my_plane * CORES + (1 - my_core)
     limit_rows = lax.broadcasted_iota(i32, own_limits.shape[1:], 0)
-    loads[1].wait()
+    for i in (1, 10, 11, 12):
+        loads[i].wait()
 
     def page_copies(d):
         return (
@@ -269,16 +295,19 @@
         first = isinstance(i, int) and i == 0
         d = source(i)
         if not first:
-            for copy in query_copies(d, d, 0):
+            for copy in plane_copies(d, i, True):
                 copy.wait_recv()
         for copy in page_copies(d):
             copy.wait_recv()
-        if not first and isinstance(i, int) and i == 1:
-            send_part(0)
-        query = queries[d]
-        tail = tails[d].astype(f32)
+        query = queries[d].reshape(query_count, CKV)
+        tail = [tails[d, x].astype(f32) for x in range(planes)]
         tail = jnp.concatenate(
-            [tail[:, : latent_width - CKV], tail[:, latent_width - CKV :]], axis=0
+            [
+                item
+                for pair in tail
+                for item in (pair[:, : latent_width - CKV], pair[:, latent_width - CKV :])
+            ],
+            axis=0,
         ).astype(bf16)
         keys, visible = [], []
         for pages_ref, limits_ref in ((own_pages, own_limits), (peer_pages, peer_limits)):
@@ -329,18 +358,28 @@
         for p in range(dp):
             part[i, p, :, :CKV] = value[p * block : (p + 1) * block].astype(bf16)
             part[i, p, :, CKV:] = stat[p * block : (p + 1) * block].astype(bf16)
-        if not first:
-            send_part(i)
+        send_part(i)
         part_recv[d, my_rank] = part[i, my_rank]
         return carry
 
+    def forward(i, carry):
+        d = source(i)
+        for copy in query_copies(d, d, 0):
+            copy.wait_recv()
+        for copy in plane_copies(d, i, False):
+            copy.start()
+        return carry
+
+    def for_others(step):
+        if dp <= 4:
+            for i in range(1, dp):
+                step(i, 0)
+        else:
+            lax.fori_loop(1, dp, step, 0)
+
     attend(0, 0)
-    if dp <= 4:
-        for i in range(1, dp):
-            attend(i, 0)
-    else:
-        send_part(0)
-        lax.fori_loop(1, dp, attend, 0)
+    for_others(forward)
+    for_others(attend)
 
     levels = []
     for d in range(dp):
@@ -415,44 +454,56 @@
 
     loads[3].wait()
     loads[6].wait()
-    own_row = lax.broadcasted_iota(i32, (rows, width), 0) // steps == my_rank
-    whole = jnp.where(
-        own_row, jnp.concatenate([residual[...].astype(f32)] * dp, axis=0), 0.0
-    ) + jnp.dot(values, out_proj[...], preferred_element_type=f32)
-    op_buf[my_rank] = whole.astype(bf16)
-    op_copies = []
-    for j, peer in enumerate(ranks):
-        item = op_buf.at[my_rank]
-        copy = to({"dp": peer}, item, item, op_send.at[j], op_recv.at[my_rank])
-        copy.start()
-        op_copies.append(copy)
-    for peer in ranks:
-        item = op_buf.at[peer]
-        to({"dp": peer}, item, item, op_send.at[0], op_recv.at[peer]).wait_recv()
-        whole += op_buf[peer].astype(f32)
-    for d in range(dp):
-        mixed[d] = whole[d * steps : (d + 1) * steps]
-    sq_buf[my_column] = jnp.broadcast_to(
-        jnp.sum(whole * whole, axis=1, keepdims=True), (rows, 128)
-    )
-    sq_copies = spread(sq_buf.at[my_column], sq_buf.at[my_column], sq_send, sq_recv)
+    own_row = lax.broadcasted_iota(i32, (rows, 1), 0) // steps == my_rank
+    kept = jnp.concatenate([residual[...].astype(f32)] * dp, axis=0)
+    split = op_first.shape[2]
+    spans = ((0, split, op_first), (split, width, op_second))
+    parts, op_copies = [], []
+    for n, (begin, end, buffer) in enumerate(spans):
+        piece = jnp.where(own_row, kept[:, begin:end], 0.0) + jnp.dot(
+            values, out_proj[:, begin:end], preferred_element_type=f32
+        )
+        buffer[my_rank] = piece.astype(bf16)
+        parts.append(piece)
+        for j, peer in enumerate(ranks):
+            item = buffer.at[my_rank]
+            copy = to({"dp": peer}, item, item, op_send.at[n, j], op_recv.at[n, my_rank])
+            copy.start()
+            op_copies.append(copy)
     loads[4].wait()
-    scaled = (whole * gain[...].reshape(1, width)).astype(bf16)
-
+    gains = gain[...].reshape(1, width)
     chunks, chunk = gu_buf.shape[1], gu_buf.shape[4]
     loads[7].wait()
     loads[8].wait()
+    squares = jnp.zeros((rows, 1), f32)
     gu_copies = []
-    for c in range(chunks):
-        at = slice(c * chunk, (c + 1) * chunk)
-        gu_buf[my_column, c, 0] = jnp.dot(
-            scaled, w_gate[:, at], preferred_element_type=f32
-        ).astype(bf16)
-        gu_buf[my_column, c, 1] = jnp.dot(
-            scaled, w_up[:, at], preferred_element_type=f32
-        ).astype(bf16)
-        item = gu_buf.at[my_column, c]
-        gu_copies.append(spread(item, item, gu_send.at[c], gu_recv.at[c]))
+    for n, (begin, end, buffer) in enumerate(spans):
+        piece = parts[n]
+        for peer in ranks:
+            item = buffer.at[peer]
+            to({"dp": peer}, item, item, op_send.at[n, 0], op_recv.at[n, peer]).wait_recv()
+            piece += buffer[peer].astype(f32)
+        for d in range(dp):
+            mixed[d, :, begin:end] = piece[d * steps : (d + 1) * steps]
+        squares += jnp.sum(piece * piece, axis=1, keepdims=True)
+        scaled = (piece * gains[:, begin:end]).astype(bf16)
+        last = n == len(spans) - 1
+        if last:
+            sq_buf[my_column] = jnp.broadcast_to(squares, (rows, 128))
+            sq_copies = spread(sq_buf.at[my_column], sq_buf.at[my_column], sq_send, sq_recv)
+        for c in range(chunks):
+            at = slice(c * chunk, (c + 1) * chunk)
+            for m, weight in enumerate((w_gate, w_up)):
+                total = jnp.dot(scaled, weight[begin:end, at], preferred_element_type=f32)
+                if n > 0:
+                    total += gu_sum[m, :, at]
+                if last:
+                    gu_buf[my_column, c, m] = total.astype(bf16)
+                else:
+                    gu_sum[m, :, at] = total
+            if last:
+                item = gu_buf.at[my_column, c]
+                gu_copies.append(spread(item, item, gu_send.at[c], gu_recv.at[c]))
 
     for copy in sq_copies:
         copy.wait()
@@ -497,6 +548,9 @@
     for d in range(dp):
         for copy in page_copies(d):
             copy.wait_send()
+        if d > 0:
+            for copy in plane_copies(d, d, False):
+                copy.wait_send()
         to(
             {"dp": ranks[0]},
             part.at[d, pl.ds(0, dp - 1)],
@@ -512,7 +566,7 @@
         result += down_recv[peer].astype(f32)
     for copy in dn_copies:
         copy.wait_send()
-    out_ref[...] = result
+    out_ref[...] = result.astype(bf16)
 
 
 def layer(
@@ -540,17 +594,22 @@
     half = up_value.shape[0] // CORES
     block = half * steps
     query_count = dp * block
+    planes = rep // CORES
+    share = query_count // planes
     vdim = up_value.shape[2]
+    split = width // 2 // 256 * 256
     chunks = hidden_width // (512 if hidden_width % 512 == 0 else 128)
     dma = pltpu.SemaphoreType.DMA
-    smem = pl.BlockSpec(memory_space=pltpu.SMEM)
-    hbm = pl.BlockSpec(memory_space=pl.ANY)
+    hbm = pl.BlockSpec(memory_space=pltpu.HBM)
     return pl.pallas_call(
         functools.partial(layer_kernel, dp, rep),
-        out_shape=jax.ShapeDtypeStruct((steps, width), f32),
-        in_specs=[smem] * 3 + [hbm] * 10,
+        out_shape=jax.ShapeDtypeStruct((steps, width), bf16),
+        in_specs=[hbm] * 13,
         out_specs=pl.BlockSpec(memory_space=pltpu.VMEM),
         scratch_shapes=[
+            pltpu.SMEM(page_rank.shape, i32),
+            pltpu.SMEM(page_index.shape, i32),
+            pltpu.SMEM(lengths.shape[::-1], i32),
             pltpu.VMEM(queries.shape, bf16),
             pltpu.VMEM(new_latent.shape, bf16),
             pltpu.VMEM(residual.shape, bf16),
@@ -561,8 +620,8 @@
             pltpu.VMEM(w_gate.shape, bf16),
             pltpu.VMEM(w_up.shape, bf16),
             pltpu.VMEM(w_down.shape, bf16),
-            pltpu.VMEM((dp, query_count, CKV), bf16),
-            pltpu.VMEM((dp, query_count // 2, 2 * (latent_width - CKV)), bf16),
+            pltpu.VMEM((dp, planes, share, CKV), bf16),
+            pltpu.VMEM((dp, planes, share // 2, 2 * (latent_width - CKV)), bf16),
             pltpu.VMEM((dp, cap) + latent_store.shape[2:], bf16),
             pltpu.VMEM((dp, cap) + latent_store.shape[2:], bf16),
             pltpu.VMEM((dp, 8, PAGE), i32),
@@ -572,17 +631,21 @@
             pltpu.VMEM((query_count, CKV), f32),
             pltpu.VMEM((rep, rows, half * vdim), bf16),
             pltpu.VMEM((rep, rows, 128), f32),
-            pltpu.VMEM((dp, rows, width), bf16),
+            pltpu.VMEM((dp, rows, split), bf16),
+            pltpu.VMEM((dp, rows, width - split), bf16),
             pltpu.VMEM((dp, steps, width), f32),
             pltpu.VMEM((rep, rows, 128), f32),
+            pltpu.VMEM((2, rows, hidden_width), f32),
             pltpu.VMEM((rep, chunks, 2, rows, hidden_width // chunks), bf16),
             pltpu.VMEM((dp, steps, width), bf16),
             pltpu.VMEM((dp, steps, width), bf16),
-            dma((10,)),
+            dma((13,)),
             dma((dp - 1,)),
             dma((dp,)),
             dma((dp - 1,)),
             dma((dp,)),
+            dma((2, dp, planes - 1)),
+            dma((2, dp, planes - 1)),
             dma((dp,)),
             dma((dp,)),
             dma((dp,)),
@@ -591,8 +654,8 @@
             dma((dp,)),
             dma((2, rep - 1)),
             dma((2, rep - 1)),
-            dma((dp - 1,)),
-            dma((dp,)),
+            dma((2, dp - 1)),
+            dma((2, dp)),
             dma((rep - 1,)),
             dma((rep - 1,)),
             dma((chunks, rep - 1)),
@@ -601,9 +664,12 @@
             dma((dp,)),
         ],
         compiler_params=pltpu.CompilerParams(
-            collective_id=0, has_side_effects=True, vmem_limit_bytes=60 * 1024 * 1024
+            collective_id=0, has_side_effects=True, vmem_limit_bytes=52 * 1024 * 1024
         ),
     )(
+        *(
+            pltpu.with_memory_space_constraint(item, pltpu.HBM)
+            for item in (
         page_rank,
         page_index,
         lengths.T,
@@ -617,7 +683,9 @@
         w_gate,
         w_up,
         w_down,
-    ).astype(bf16)
+            )
+        )
+    )
 
 
 def solution(mesh):

time: 44 us -> 40.5 us (0.920)
  Pallas kernels: 42.5 us -> 39.8 us
  other arithmetic: 1.31 us -> 0 us
  local copies, waits for them, and re-layouts: 0 us -> 0.6 us
    pallas_call x1, Pallas kernels: 42.5 us -> 39.8 us  [layer(): pl.pallas_call(functools.partial(layer_kernel, dp, rep), out_shape=jax.Sh...]
    convert_element_type x1 -> x0, other arithmetic: 1.31 us -> none  [layer(): return pl.pallas_call(functools.partial(layer_kernel, dp, rep), out_shape...]
    unnamed x0 -> x1, local copies, waits for them, and re-layouts: none -> 0.6 us
where the time goes in v3:
time: 40.5 us; the launch traced here: 40.4 us
  Pallas kernels  39.8 us (98%)
  local copies, waits for them, and re-layouts  0.6 us (1%)
    pallas_call x1, Pallas kernels, layer(): pl.pallas_call(functools.partial(layer_kernel, dp, rep), out_shape=jax.Sh...  39.8 us

profile of v3, /device:TPU:0, one launch (start us, length us, event | category | flops | bytes accessed | tf_op | source)
XLA Modules:
  0.0 40.4 jit_solution(10643084952947345377)
XLA Ops:
  0.0 39.8 %shard_map.127 = bf16[2,1792]{1,0:T(2,128)(2,1)S(1)} custom-call(s32[4,12]{1,0:T(4,128)} %page_rank_hbm.1, s32[4,12]{1,0:T(4,128)} %page_index_hbm.1, s32[1,4]{1,0:T(1,128)} %bitcast.1, bf16[2,36864]{1,0:T(2,128)(2,1)} %queries_hbm.1, bf16[2,576]{1,0:T(2,128)(2,1)} %fresh_hbm.1, bf16[2,1792]{1,0:T(2,128)(2,1)} %residual_hbm.1, f32[1792]{0:T(1024)} %gain_hbm.1, ...), custom_call_target="tpu_custom_call" | custom-call | tf_op jit(solution)/shard_map/pallas_call | solution.py:604
  39.8 0.6 %copy.15 = bf16[2,1792]{1,0:T(2,128)(2,1)} copy(bf16[2,1792]{1,0:T(2,128)(2,1)S(1)} %shard_map.127) | data formatting | bytes 14336

commit v4 on v3

--- a/solution.py
+++ b/solution.py
@@ -64,10 +64,12 @@
     tails,
     own_pages,
     peer_pages,
-    own_limits,
-    peer_limits,
+    turned,
     part,
     part_recv,
+    stat_sum,
+    stat_part,
+    stat_recv,
     latent,
     value_buf,
     level_buf,
@@ -82,26 +84,17 @@
     load_sem,
     q_send,
     q_recv,
-    t_send,
-    t_recv,
     x_send,
     x_recv,
-    pg_send,
-    pg_recv,
-    lm_send,
-    lm_recv,
-    p_send,
-    p_recv,
-    v_send,
-    v_recv,
-    op_send,
-    op_recv,
-    sq_send,
-    sq_recv,
+    pg_sem,
+    p_sem,
+    st_sem,
+    v_sem,
+    op_sem,
+    sq_sem,
     gu_send,
     gu_recv,
-    dn_send,
-    dn_recv,
+    dn_sem,
 ):
     my_rank = lax.axis_index("dp")
     my_column = lax.axis_index("rep")
@@ -167,14 +160,12 @@
             device_id_type=MESH,
         )
 
-    def spread(start, end, send, recv):
-        copies = [
-            to({"rep": peer}, start, end, send.at[k], recv.at[k])
-            for k, peer in enumerate(columns)
-        ]
-        for copy in copies:
-            copy.start()
-        return copies
+    def send_all(axis, start, end, send, recv):
+        for peer in ranks if axis == "dp" else columns:
+            to({axis: peer}, start, end, send, recv).start()
+
+    def arrived(buffer, sem):
+        pltpu.make_async_copy(buffer, buffer, sem).wait()
 
     loads[0].wait()
     pieces = []
@@ -205,13 +196,19 @@
 
     pl.semaphore_wait(barrier, dp - 1 + rep - 1)
 
-    def query_copies(peer, d, j):
+    def query_copies(peer, d, near):
         return [
-            to({"dp": peer}, item.at[d, my_plane], item.at[d, my_plane], send.at[j], recv.at[d])
-            for item, send, recv in ((queries, q_send, q_recv), (tails, t_send, t_recv))
+            to(
+                {"dp": peer},
+                item.at[d] if near else item.at[d, my_plane],
+                item.at[d] if near else item.at[d, my_plane],
+                q_send.at[2 * near + n],
+                q_recv.at[n, d],
+            )
+            for n, item in enumerate((queries, tails))
         ]
 
-    def plane_copies(d, i, arriving):
+    def plane_copies(d, arriving):
         copies = []
         for j in range(1, planes):
             peer = lax.rem(my_plane + j, planes) * CORES + my_core
@@ -222,30 +219,22 @@
                         {"rep": peer},
                         item.at[d, x],
                         item.at[d, x],
-                        x_send.at[n, i, j - 1],
+                        x_send.at[n],
                         x_recv.at[n, d, j - 1],
                     )
                 )
         return copies
 
-    q_copies = []
-    for j, peer in enumerate(ranks):
-        for copy in query_copies(peer, my_rank, j):
+    for j, peer in (*enumerate(ranks[1:], 1), (0, ranks[0])):
+        for copy in query_copies(peer, my_rank, int(j == 0)):
             copy.start()
-            q_copies.append(copy)
 
     partner = my_plane * CORES + (1 - my_core)
-    limit_rows = lax.broadcasted_iota(i32, own_limits.shape[1:], 0)
     for i in (1, 10, 11, 12):
         loads[i].wait()
 
-    def page_copies(d):
-        return (
-            to({"rep": partner}, own_pages.at[d], peer_pages.at[d], pg_send.at[d], pg_recv.at[d]),
-            to(
-                {"rep": partner}, own_limits.at[d], peer_limits.at[d], lm_send.at[d], lm_recv.at[d]
-            ),
-        )
+    def page_copy(d):
+        return to({"rep": partner}, own_pages.at[d], peer_pages.at[d], pg_sem.at[0], pg_sem.at[1 + d])
 
     def compact(i, carry):
         d = source(i)
@@ -261,13 +250,12 @@
                 index[j] = index[j] + hit * page_index[d, q]
                 limit[j] = limit[j] + hit * seen
             count = count + held
-        levels = jnp.zeros(limit_rows.shape, i32)
         for j in range(cap):
-            own_pages[d, j] = pages[index[j]]
-            levels = jnp.where(limit_rows == j, limit[j], levels)
-        own_limits[d] = levels
-        for copy in page_copies(d):
-            copy.start()
+            own_pages[d, j, :latent_width] = pages[index[j]]
+            own_pages[d, j, latent_width:] = jnp.full(
+                (own_pages.shape[2] - latent_width, PAGE), limit[j].astype(f32)
+            ).astype(bf16)
+        page_copy(d).start()
         return carry
 
     compact(0, 0)
@@ -280,128 +268,150 @@
     lanes = lax.broadcasted_iota(i32, (query_count, PAGE), 1)
     row_ids = lax.broadcasted_iota(i32, (query_count, PAGE), 0)
 
-    def send_part(i):
+    def prepare(i, carry):
         d = source(i)
-        for peer in ranks:
-            to(
-                {"dp": peer},
-                part.at[i, peer],
-                part_recv.at[d, my_rank],
-                p_send.at[i],
-                p_recv.at[d],
-            ).start()
-
-    def attend(i, carry):
-        first = isinstance(i, int) and i == 0
-        d = source(i)
-        if not first:
-            for copy in plane_copies(d, i, True):
+        page_copy(d).wait_recv()
+        for n, pages_ref in enumerate((own_pages, peer_pages)):
+            for j in range(cap):
+                at = (n * cap + j) * PAGE
+                turned[d, at : at + PAGE] = pages_ref[d, j, :CKV].T
+        return carry
+
+    def attend_all(group, first=False, near=False):
+        ranks_here = [source(i) for i in group]
+        for d in () if first else ranks_here:
+            for copy in query_copies(d, d, 1) if near else plane_copies(d, True):
                 copy.wait_recv()
-        for copy in page_copies(d):
-            copy.wait_recv()
-        query = queries[d].reshape(query_count, CKV)
-        tail = [tails[d, x].astype(f32) for x in range(planes)]
-        tail = jnp.concatenate(
-            [
-                item
-                for pair in tail
-                for item in (pair[:, : latent_width - CKV], pair[:, latent_width - CKV :])
-            ],
-            axis=0,
-        ).astype(bf16)
-        keys, visible = [], []
-        for pages_ref, limits_ref in ((own_pages, own_limits), (peer_pages, peer_limits)):
-            for j in range(cap):
-                keys.append(pages_ref[d, j])
-                visible.append(lanes < limits_ref[d, j : j + 1, :])
-        keys = jnp.concatenate(keys, axis=1)
-        score = (
-            jnp.dot(query, keys[:CKV], preferred_element_type=f32)
-            + jnp.dot(tail, keys[CKV:], preferred_element_type=f32)
-        ) * score_scale
-        scores = [
-            jnp.where(see, score[:, n * PAGE : (n + 1) * PAGE], mask_value)
-            for n, see in enumerate(visible)
-        ]
-        if first:
-            loads[2].wait()
-            fresh = jnp.concatenate(
-                [fresh_raw[...].astype(f32), jnp.zeros((PAGE - steps, latent_width), f32)], axis=0
+        results = []
+        for d in ranks_here:
+            query = queries[d].reshape(query_count, CKV)
+            tail = [tails[d, x].astype(f32) for x in range(planes)]
+            tail = jnp.concatenate(
+                [
+                    item
+                    for pair in tail
+                    for item in (pair[:, : latent_width - CKV], pair[:, latent_width - CKV :])
+                ],
+                axis=0,
             ).astype(bf16)
-            across = (((1,), (1,)), ((), ()))
-            extra = lax.dot_general(
-                query, fresh[:, :CKV], across, preferred_element_type=f32
-            ) + lax.dot_general(tail, fresh[:, CKV:], across, preferred_element_type=f32)
-            step = lax.rem(row_ids, block) // half
-            see = lanes + PAGE * my_plane <= step
-            visible.append(see)
-            scores.append(jnp.where(see, extra * score_scale, mask_value))
-        peak = jnp.max(functools.reduce(jnp.maximum, scores), axis=1, keepdims=True)
-        weights = [
-            jnp.where(see, jnp.exp(score - peak), 0.0)
-            for see, score in zip(visible, scores, strict=True)
-        ]
-        total = jnp.sum(functools.reduce(jnp.add, weights), axis=1, keepdims=True)
-        rounded = [weight.astype(bf16) for weight in weights]
-        value = lax.dot_general(
-            jnp.concatenate(rounded[: CORES * cap], axis=1),
-            keys[:CKV],
-            (((1,), (1,)), ((), ())),
-            preferred_element_type=f32,
-        )
-        if first:
-            value += jnp.dot(rounded[-1], fresh[:, :CKV], preferred_element_type=f32)
-        value = value / jnp.maximum(total, tiny)
-        level = jnp.where(total > 0.0, peak + jnp.log(jnp.maximum(total, tiny)), mask_value)
-        one, two, three = (term.astype(f32) for term in split_three(level))
-        stat = jnp.where(lanes == 0, one, jnp.where(lanes == 1, two, three))
-        for p in range(dp):
-            part[i, p, :, :CKV] = value[p * block : (p + 1) * block].astype(bf16)
-            part[i, p, :, CKV:] = stat[p * block : (p + 1) * block].astype(bf16)
-        send_part(i)
-        part_recv[d, my_rank] = part[i, my_rank]
-        return carry
+            keys, visible = [], []
+            for pages_ref in (own_pages, peer_pages):
+                for j in range(cap):
+                    keys.append(pages_ref[d, j, :latent_width])
+                    limit = pages_ref[d, j, latent_width:].astype(f32)[:1]
+                    visible.append(lanes < limit.astype(i32))
+            keys = jnp.concatenate(keys, axis=1)
+            score = (
+                jnp.dot(query, keys[:CKV], preferred_element_type=f32)
+                + jnp.dot(tail, keys[CKV:], preferred_element_type=f32)
+            ) * score_scale
+            scores = [
+                jnp.where(see, score[:, n * PAGE : (n + 1) * PAGE], mask_value)
+                for n, see in enumerate(visible)
+            ]
+            if first:
+                fresh = jnp.concatenate(
+                    [fresh_raw[...].astype(f32), jnp.zeros((PAGE - steps, latent_width), f32)],
+                    axis=0,
+                ).astype(bf16)
+                across = (((1,), (1,)), ((), ()))
+                extra = lax.dot_general(
+                    query, fresh[:, :CKV], across, preferred_element_type=f32
+                ) + lax.dot_general(tail, fresh[:, CKV:], across, preferred_element_type=f32)
+                step = lax.rem(row_ids, block) // half
+                see = lanes + PAGE * my_plane <= step
+                visible.append(see)
+                scores.append(jnp.where(see, extra * score_scale, mask_value))
+            peak = jnp.max(functools.reduce(jnp.maximum, scores), axis=1, keepdims=True)
+            weights = [
+                jnp.where(see, jnp.exp(score - peak), 0.0)
+                for see, score in zip(visible, scores, strict=True)
+            ]
+            total = jnp.sum(functools.reduce(jnp.add, weights), axis=1, keepdims=True)
+            rounded = [weight.astype(bf16) for weight in weights]
+            value = jnp.dot(
+                jnp.concatenate(rounded[: CORES * cap], axis=1),
+                turned[d],
+                preferred_element_type=f32,
+            )
+            if first:
+                value += jnp.dot(rounded[-1], fresh[:, :CKV], preferred_element_type=f32)
+            value = value * (1.0 / jnp.maximum(total, tiny))
+            level = jnp.where(
+                total > 0.0, peak + jnp.log(jnp.maximum(total, tiny)), mask_value
+            )
+            results.append((value, level))
+        for i, d, (value, level) in zip(group, ranks_here, results, strict=True):
+            for p in range(dp):
+                part[i, p] = value[p * block : (p + 1) * block].astype(bf16)
+            for peer in ranks:
+                to(
+                    {"dp": peer},
+                    part.at[i, peer],
+                    part_recv.at[d, my_rank],
+                    p_sem.at[0],
+                    p_sem.at[1],
+                ).start()
+            part_recv[d, my_rank] = part[i, my_rank]
+        stat = jnp.zeros((query_count, PAGE), f32) if first else stat_sum[...]
+        for d, (value, level) in zip(ranks_here, results, strict=True):
+            for n, term in enumerate(split_three(level)):
+                stat = jnp.where(lanes == 3 * d + n, term.astype(f32), stat)
+        stat_sum[...] = stat
 
     def forward(i, carry):
         d = source(i)
         for copy in query_copies(d, d, 0):
             copy.wait_recv()
-        for copy in plane_copies(d, i, False):
+        for copy in plane_copies(d, False):
             copy.start()
         return carry
 
-    def for_others(step):
-        if dp <= 4:
-            for i in range(1, dp):
-                step(i, 0)
-        else:
-            lax.fori_loop(1, dp, step, 0)
-
-    attend(0, 0)
-    for_others(forward)
-    for_others(attend)
+    prepare(0, 0)
+    loads[2].wait()
+    attend_all((0,), first=True)
+    if dp == 4:
+        prepare(1, 0)
+        for i in range(2, dp):
+            forward(i, 0)
+        attend_all((1,), near=True)
+        for i in range(2, dp):
+            prepare(i, 0)
+        for i in range(2, dp):
+            attend_all((i,))
+    else:
+
+        def attend(i, carry):
+            attend_all((i,))
+            return carry
+
+        lax.fori_loop(2, dp, forward, 0)
+        lax.fori_loop(1, dp, prepare, 0)
+        attend_all((1,), near=True)
+        lax.fori_loop(2, dp, attend, 0)
+    for p in range(dp):
+        stat_part[p] = stat_sum[p * block : (p + 1) * block].astype(bf16)
+    for j, peer in enumerate(ranks):
+        to(
+            {"dp": peer}, stat_part.at[peer], stat_recv.at[my_rank], st_sem.at[0], st_sem.at[1]
+        ).start()
+    stat_recv[my_rank] = stat_part[my_rank]
 
     levels = []
-    for d in range(dp):
-        to(
-            {"dp": ranks[0]},
-            part.at[0, pl.ds(0, dp - 1)],
-            part_recv.at[d, pl.ds(0, dp - 1)],
-            p_send.at[0],
-            p_recv.at[d],
-        ).wait_recv()
+    others = pl.ds(0, dp - 1)
+    arrived(part_recv.at[others], p_sem.at[1])
+    arrived(stat_recv.at[others], st_sem.at[1])
+    stat = stat_recv[...].astype(f32)
     for d in range(dp):
         message = part_recv[d].astype(f32)
-        level = (
-            message[:, :, CKV : CKV + 1]
-            + message[:, :, CKV + 1 : CKV + 2]
-            + message[:, :, CKV + 2 : CKV + 3]
+        level = functools.reduce(
+            jnp.add, [stat[:, :, 3 * d + n : 3 * d + n + 1] for n in range(3)]
         )
         best = jnp.max(level, axis=0)
         factor = jnp.exp(level - best[None])
         total = jnp.sum(factor, axis=0)
         latent[d * block : (d + 1) * block] = (
-            jnp.sum(message[:, :, :CKV] * factor, axis=0) / total
+            jnp.sum(message * (factor / total[None]), axis=0)
         )
         levels.append(best + jnp.log(total))
     loads[5].wait()
@@ -428,10 +438,11 @@
         level = jnp.sum(level.reshape(rows, half, 128), axis=1)
     value_buf[my_column] = picked.astype(bf16)
     level_buf[my_column] = level
-    v_copies = spread(value_buf.at[my_column], value_buf.at[my_column], v_send.at[0], v_recv.at[0])
-    v_copies += spread(level_buf.at[my_column], level_buf.at[my_column], v_send.at[1], v_recv.at[1])
-    for copy in v_copies:
-        copy.wait()
+    send_all("rep", value_buf.at[my_column], value_buf.at[my_column], v_sem.at[0], v_sem.at[1])
+    send_all("rep", level_buf.at[my_column], level_buf.at[my_column], v_sem.at[2], v_sem.at[3])
+    columns_here = pl.ds(0, rep - 1)
+    for n, item in ((1, value_buf), (3, level_buf)):
+        arrived(item.at[columns_here], v_sem.at[n])
     values = []
     for k in range(CORES):
         held = range(k, rep, CORES)
@@ -458,30 +469,25 @@
     kept = jnp.concatenate([residual[...].astype(f32)] * dp, axis=0)
     split = op_first.shape[2]
     spans = ((0, split, op_first), (split, width, op_second))
-    parts, op_copies = [], []
+    parts = []
     for n, (begin, end, buffer) in enumerate(spans):
         piece = jnp.where(own_row, kept[:, begin:end], 0.0) + jnp.dot(
             values, out_proj[:, begin:end], preferred_element_type=f32
         )
         buffer[my_rank] = piece.astype(bf16)
         parts.append(piece)
-        for j, peer in enumerate(ranks):
-            item = buffer.at[my_rank]
-            copy = to({"dp": peer}, item, item, op_send.at[n, j], op_recv.at[n, my_rank])
-            copy.start()
-            op_copies.append(copy)
+        item = buffer.at[my_rank]
+        send_all("dp", item, item, op_sem.at[0, n], op_sem.at[1, n])
     loads[4].wait()
     gains = gain[...].reshape(1, width)
     chunks, chunk = gu_buf.shape[1], gu_buf.shape[4]
     loads[7].wait()
     loads[8].wait()
     squares = jnp.zeros((rows, 1), f32)
-    gu_copies = []
     for n, (begin, end, buffer) in enumerate(spans):
         piece = parts[n]
+        arrived(buffer.at[others], op_sem.at[1, n])
         for peer in ranks:
-            item = buffer.at[peer]
-            to({"dp": peer}, item, item, op_send.at[n, 0], op_recv.at[n, peer]).wait_recv()
             piece += buffer[peer].astype(f32)
         for d in range(dp):
             mixed[d, :, begin:end] = piece[d * steps : (d + 1) * steps]
@@ -490,7 +496,8 @@
         last = n == len(spans) - 1
         if last:
             sq_buf[my_column] = jnp.broadcast_to(squares, (rows, 128))
-            sq_copies = spread(sq_buf.at[my_column], sq_buf.at[my_column], sq_send, sq_recv)
+            item = sq_buf.at[my_column]
+            send_all("rep", item, item, sq_sem.at[0], sq_sem.at[1])
         for c in range(chunks):
             at = slice(c * chunk, (c + 1) * chunk)
             for m, weight in enumerate((w_gate, w_up)):
@@ -503,10 +510,9 @@
                     gu_sum[m, :, at] = total
             if last:
                 item = gu_buf.at[my_column, c]
-                gu_copies.append(spread(item, item, gu_send.at[c], gu_recv.at[c]))
-
-    for copy in sq_copies:
-        copy.wait()
+                send_all("rep", item, item, gu_send, gu_recv.at[c])
+
+    arrived(sq_buf.at[columns_here], sq_sem.at[1])
     total = sq_buf[0]
     for c in range(1, rep):
         total += sq_buf[c]
@@ -514,8 +520,7 @@
     loads[9].wait()
     down = jnp.zeros((rows, width), f32)
     for c in range(chunks):
-        for copy in gu_copies[c]:
-            copy.wait()
+        arrived(gu_buf.at[columns_here, c], gu_recv.at[c])
         gate = gu_buf[0, c, 0].astype(f32)
         up = gu_buf[0, c, 1].astype(f32)
         for other in range(1, rep):
@@ -529,43 +534,34 @@
         )
     for d in range(dp):
         down_send[d] = down[d * steps : (d + 1) * steps].astype(bf16)
-    dn_copies = [
+    for peer in ranks:
         to(
             {"dp": peer},
             down_send.at[peer],
             down_recv.at[my_rank],
-            dn_send.at[k],
-            dn_recv.at[my_rank],
-        )
-        for k, peer in enumerate(ranks)
-    ]
-    for copy in dn_copies:
-        copy.start()
+            dn_sem.at[0],
+            dn_sem.at[1],
+        ).start()
     result = mixed[my_rank] + down_send[my_rank].astype(f32)
 
-    for copy in q_copies + op_copies:
-        copy.wait_send()
-    for d in range(dp):
-        for copy in page_copies(d):
-            copy.wait_send()
-        if d > 0:
-            for copy in plane_copies(d, d, False):
-                copy.wait_send()
-        to(
-            {"dp": ranks[0]},
-            part.at[d, pl.ds(0, dp - 1)],
-            part_recv.at[0, pl.ds(0, dp - 1)],
-            p_send.at[d],
-            p_recv.at[0],
-        ).wait_send()
-
+    for n, item in enumerate((queries, tails)):
+        arrived(item.at[pl.ds(0, dp - 2), 0], q_send.at[n])
+        arrived(item.at[0], q_send.at[2 + n])
+        arrived(item.at[pl.ds(0, dp - 2), pl.ds(0, planes - 1)], x_send.at[n])
+    arrived(own_pages, pg_sem.at[0])
+    arrived(part.at[others], p_sem.at[0])
+    arrived(stat_part.at[others], st_sem.at[0])
+    for n, item in ((0, value_buf), (2, level_buf)):
+        arrived(item.at[columns_here], v_sem.at[n])
+    for n, item in enumerate((op_first, op_second)):
+        arrived(item.at[others], op_sem.at[0, n])
+    arrived(sq_buf.at[columns_here], sq_sem.at[0])
+    arrived(gu_buf.at[columns_here], gu_send)
+
+    arrived(down_recv.at[others], dn_sem.at[1])
     for peer in ranks:
-        to(
-            {"dp": peer}, down_send.at[peer], down_recv.at[peer], dn_send.at[0], dn_recv.at[peer]
-        ).wait_recv()
         result += down_recv[peer].astype(f32)
-    for copy in dn_copies:
-        copy.wait_send()
+    arrived(down_send.at[others], dn_sem.at[0])
     out_ref[...] = result.astype(bf16)
 
 
@@ -622,12 +618,14 @@
             pltpu.VMEM(w_down.shape, bf16),
             pltpu.VMEM((dp, planes, share, CKV), bf16),
             pltpu.VMEM((dp, planes, share // 2, 2 * (latent_width - CKV)), bf16),
-            pltpu.VMEM((dp, cap) + latent_store.shape[2:], bf16),
-            pltpu.VMEM((dp, cap) + latent_store.shape[2:], bf16),
-            pltpu.VMEM((dp, 8, PAGE), i32),
-            pltpu.VMEM((dp, 8, PAGE), i32),
-            pltpu.VMEM((dp, dp, block, CKV + PAGE), bf16),
-            pltpu.VMEM((dp, dp, block, CKV + PAGE), bf16),
+            pltpu.VMEM((dp, cap, latent_width + 16, PAGE), bf16),
+            pltpu.VMEM((dp, cap, latent_width + 16, PAGE), bf16),
+            pltpu.VMEM((dp, CORES * cap * PAGE, CKV), bf16),
+            pltpu.VMEM((dp, dp, block, CKV), bf16),
+            pltpu.VMEM((dp, dp, block, CKV), bf16),
+            pltpu.VMEM((query_count, PAGE), f32),
+            pltpu.VMEM((dp, block, PAGE), bf16),
+            pltpu.VMEM((dp, block, PAGE), bf16),
             pltpu.VMEM((query_count, CKV), f32),
             pltpu.VMEM((rep, rows, half * vdim), bf16),
             pltpu.VMEM((rep, rows, 128), f32),
@@ -640,31 +638,22 @@
             pltpu.VMEM((dp, steps, width), bf16),
             pltpu.VMEM((dp, steps, width), bf16),
             dma((13,)),
-            dma((dp - 1,)),
-            dma((dp,)),
-            dma((dp - 1,)),
-            dma((dp,)),
+            dma((4,)),
+            dma((2, dp)),
+            dma((2,)),
             dma((2, dp, planes - 1)),
-            dma((2, dp, planes - 1)),
-            dma((dp,)),
-            dma((dp,)),
-            dma((dp,)),
-            dma((dp,)),
-            dma((dp,)),
-            dma((dp,)),
-            dma((2, rep - 1)),
-            dma((2, rep - 1)),
-            dma((2, dp - 1)),
-            dma((2, dp)),
-            dma((rep - 1,)),
-            dma((rep - 1,)),
-            dma((chunks, rep - 1)),
-            dma((chunks, rep - 1)),
-            dma((dp - 1,)),
-            dma((dp,)),
+            dma((1 + dp,)),
+            dma((2,)),
+            dma((2,)),
+            dma((4,)),
+            dma((2, 2)),
+            dma((2,)),
+            dma(()),
+            dma((chunks,)),
+            dma((2,)),
         ],
         compiler_params=pltpu.CompilerParams(
-            collective_id=0, has_side_effects=True, vmem_limit_bytes=52 * 1024 * 1024
+            collective_id=0, has_side_effects=True, vmem_limit_bytes=53 * 1024 * 1024
         ),
     )(
         *(

time: 40.5 us -> 38.7 us (0.956)
  Pallas kernels: 39.8 us -> 38 us
    pallas_call x1, Pallas kernels: 39.8 us -> 38 us  [layer(): pl.pallas_call(functools.partial(layer_kernel, dp, rep), out_shape=jax.Sh...]
where the time goes in v4:
time: 38.7 us; the launch traced here: 38.6 us
  Pallas kernels  38 us (98%)
  local copies, waits for them, and re-layouts  0.6 us (2%)
    pallas_call x1, Pallas kernels, layer(): pl.pallas_call(functools.partial(layer_kernel, dp, rep), out_shape=jax.Sh...  38 us

profile of v4, /device:TPU:0, one launch (start us, length us, event | category | flops | bytes accessed | tf_op | source)
XLA Modules:
  0.0 38.6 jit_solution(6954742005578067476)
XLA Ops:
  0.0 38.0 %shard_map.127 = bf16[2,1792]{1,0:T(2,128)(2,1)S(1)} custom-call(s32[4,12]{1,0:T(4,128)} %page_rank_hbm.1, s32[4,12]{1,0:T(4,128)} %page_index_hbm.1, s32[1,4]{1,0:T(1,128)} %bitcast.1, bf16[2,36864]{1,0:T(2,128)(2,1)} %queries_hbm.1, bf16[2,576]{1,0:T(2,128)(2,1)} %fresh_hbm.1, bf16[2,1792]{1,0:T(2,128)(2,1)} %residual_hbm.1, f32[1792]{0:T(1024)} %gain_hbm.1, ...), custom_call_target="tpu_custom_call" | custom-call | tf_op jit(solution)/shard_map/pallas_call | solution.py:600
  38.0 0.6 %copy.15 = bf16[2,1792]{1,0:T(2,128)(2,1)} copy(bf16[2,1792]{1,0:T(2,128)(2,1)S(1)} %shard_map.127) | data formatting | bytes 14336

commit v5 on v4

--- a/solution.py
+++ b/solution.py
@@ -113,7 +113,11 @@
     vdim = up_value.shape[2]
 
     barrier = pltpu.get_barrier_semaphore()
-    columns = [lax.rem(my_column + k, rep) for k in range(1, rep)]
+    columns = [
+        lax.rem(my_plane + j, rep // CORES) * CORES + core
+        for j in (*range(1, rep // CORES), 0)
+        for core in ((my_core, 1 - my_core) if j else (1 - my_core,))
+    ]
     bits = dp.bit_length() - 1
 
     def flipped(mask):
@@ -277,15 +281,25 @@
                 turned[d, at : at + PAGE] = pages_ref[d, j, :CKV].T
         return carry
 
-    def attend_all(group, first=False, near=False):
-        ranks_here = [source(i) for i in group]
-        for d in () if first else ranks_here:
-            for copy in query_copies(d, d, 1) if near else plane_copies(d, True):
-                copy.wait_recv()
-        results = []
-        for d in ranks_here:
-            query = queries[d].reshape(query_count, CKV)
-            tail = [tails[d, x].astype(f32) for x in range(planes)]
+    def attend(group, first=False, waits=(), x=None, last=True):
+        members = [source(i) for i in group]
+        for copy in waits:
+            copy.wait_recv()
+        count = query_count if x is None else share
+        across = (((1,), (1,)), ((), ()))
+        if first:
+            fresh = jnp.concatenate(
+                [fresh_raw[...].astype(f32), jnp.zeros((PAGE - steps, latent_width), f32)],
+                axis=0,
+            ).astype(bf16)
+        raw = []
+        for d in members:
+            if x is None:
+                query = queries[d].reshape(query_count, CKV)
+                tail = [tails[d, y].astype(f32) for y in range(planes)]
+            else:
+                query = queries[d, x]
+                tail = [tails[d, x].astype(f32)]
             tail = jnp.concatenate(
                 [
                     item
@@ -294,41 +308,42 @@
                 ],
                 axis=0,
             ).astype(bf16)
-            keys, visible = [], []
-            for pages_ref in (own_pages, peer_pages):
-                for j in range(cap):
-                    keys.append(pages_ref[d, j, :latent_width])
-                    limit = pages_ref[d, j, latent_width:].astype(f32)[:1]
-                    visible.append(lanes < limit.astype(i32))
-            keys = jnp.concatenate(keys, axis=1)
-            score = (
-                jnp.dot(query, keys[:CKV], preferred_element_type=f32)
-                + jnp.dot(tail, keys[CKV:], preferred_element_type=f32)
-            ) * score_scale
-            scores = [
-                jnp.where(see, score[:, n * PAGE : (n + 1) * PAGE], mask_value)
-                for n, see in enumerate(visible)
-            ]
+            keys = jnp.concatenate(
+                [ref[d, j, :latent_width] for ref in (own_pages, peer_pages) for j in range(cap)],
+                axis=1,
+            )
+            score = jnp.dot(query, keys[:CKV], preferred_element_type=f32) + jnp.dot(
+                tail, keys[CKV:], preferred_element_type=f32
+            )
             if first:
-                fresh = jnp.concatenate(
-                    [fresh_raw[...].astype(f32), jnp.zeros((PAGE - steps, latent_width), f32)],
-                    axis=0,
-                ).astype(bf16)
-                across = (((1,), (1,)), ((), ()))
                 extra = lax.dot_general(
                     query, fresh[:, :CKV], across, preferred_element_type=f32
                 ) + lax.dot_general(tail, fresh[:, CKV:], across, preferred_element_type=f32)
+                score = jnp.concatenate([score, extra], axis=1)
+            raw.append(score)
+        weighed = []
+        for d, score in zip(members, raw, strict=True):
+            visible = []
+            for ref in (own_pages, peer_pages):
+                for j in range(cap):
+                    limit = ref[d, j, latent_width:].astype(f32)[:1]
+                    visible.append(lanes[:count] < limit.astype(i32))
+            if first:
                 step = lax.rem(row_ids, block) // half
-                see = lanes + PAGE * my_plane <= step
-                visible.append(see)
-                scores.append(jnp.where(see, extra * score_scale, mask_value))
+                visible.append(lanes + PAGE * my_plane <= step)
+            scores = [
+                jnp.where(see, score[:, n * PAGE : (n + 1) * PAGE] * score_scale, mask_value)
+                for n, see in enumerate(visible)
+            ]
             peak = jnp.max(functools.reduce(jnp.maximum, scores), axis=1, keepdims=True)
             weights = [
                 jnp.where(see, jnp.exp(score - peak), 0.0)
                 for see, score in zip(visible, scores, strict=True)
             ]
             total = jnp.sum(functools.reduce(jnp.add, weights), axis=1, keepdims=True)
-            rounded = [weight.astype(bf16) for weight in weights]
+            weighed.append((peak, total, [weight.astype(bf16) for weight in weights]))
+        outcome = []
+        for d, (peak, total, rounded) in zip(members, weighed, strict=True):
             value = jnp.dot(
                 jnp.concatenate(rounded[: CORES * cap], axis=1),
                 turned[d],
@@ -336,28 +351,41 @@
             )
             if first:
                 value += jnp.dot(rounded[-1], fresh[:, :CKV], preferred_element_type=f32)
-            value = value * (1.0 / jnp.maximum(total, tiny))
-            level = jnp.where(
-                total > 0.0, peak + jnp.log(jnp.maximum(total, tiny)), mask_value
-            )
-            results.append((value, level))
-        for i, d, (value, level) in zip(group, ranks_here, results, strict=True):
-            for p in range(dp):
-                part[i, p] = value[p * block : (p + 1) * block].astype(bf16)
-            for peer in ranks:
-                to(
-                    {"dp": peer},
-                    part.at[i, peer],
-                    part_recv.at[d, my_rank],
-                    p_sem.at[0],
-                    p_sem.at[1],
-                ).start()
-            part_recv[d, my_rank] = part[i, my_rank]
-        stat = jnp.zeros((query_count, PAGE), f32) if first else stat_sum[...]
-        for d, (value, level) in zip(ranks_here, results, strict=True):
-            for n, term in enumerate(split_three(level)):
-                stat = jnp.where(lanes == 3 * d + n, term.astype(f32), stat)
-        stat_sum[...] = stat
+            outcome.append(value * (1.0 / jnp.maximum(total, tiny)))
+
+        def send_part(i, d, p):
+            to(
+                {"dp": p},
+                part.at[i, p],
+                part_recv.at[d, my_rank],
+                p_sem.at[0],
+                p_sem.at[1],
+            ).start()
+
+        for i, d, value in zip(group, members, outcome, strict=True):
+            if x is None:
+                for p in range(dp):
+                    part[i, p] = value[p * block : (p + 1) * block].astype(bf16)
+                for peer in ranks:
+                    send_part(i, d, peer)
+            else:
+                for q in range(dp // planes):
+                    p = x * (dp // planes) + q
+                    part[i, p] = value[q * block : (q + 1) * block].astype(bf16)
+                    pl.when(p != my_rank)(functools.partial(send_part, i, d, p))
+            if last:
+                part_recv[d, my_rank] = part[i, my_rank]
+        terms = []
+        for peak, total, rounded in weighed:
+            level = jnp.where(total > 0.0, peak + jnp.log(jnp.maximum(total, tiny)), mask_value)
+            terms.append([term.astype(f32) for term in split_three(level)])
+        for y in range(planes) if x is None else (x,):
+            at = y * share if x is None else 0
+            stat = jnp.zeros((share, PAGE), f32) if first else stat_sum[y]
+            for d, items in zip(members, terms, strict=True):
+                for n, term in enumerate(items):
+                    stat = jnp.where(lanes[:share] == 3 * d + n, term[at : at + share], stat)
+            stat_sum[y] = stat
 
     def forward(i, carry):
         d = source(i)
@@ -369,28 +397,38 @@
 
     prepare(0, 0)
     loads[2].wait()
-    attend_all((0,), first=True)
+    attend((0,), first=True)
+    near_waits = query_copies(ranks[0], ranks[0], 1)
     if dp == 4:
         prepare(1, 0)
         for i in range(2, dp):
             forward(i, 0)
-        attend_all((1,), near=True)
+        attend((1,), waits=near_waits)
         for i in range(2, dp):
             prepare(i, 0)
-        for i in range(2, dp):
-            attend_all((i,))
+        attend((2, 3), x=my_plane, last=False)
+        for j in range(1, planes):
+            attend(
+                (2, 3),
+                waits=[copy for i in (2, 3) for copy in plane_copies(source(i), True)]
+                if j == 1
+                else (),
+                x=lax.rem(my_plane + planes - j, planes),
+                last=j == planes - 1,
+            )
     else:
 
-        def attend(i, carry):
-            attend_all((i,))
+        def attend_other(i, carry):
+            attend((i,), waits=plane_copies(source(i), True))
             return carry
 
         lax.fori_loop(2, dp, forward, 0)
         lax.fori_loop(1, dp, prepare, 0)
-        attend_all((1,), near=True)
-        lax.fori_loop(2, dp, attend, 0)
+        attend((1,), waits=near_waits)
+        lax.fori_loop(2, dp, attend_other, 0)
     for p in range(dp):
-        stat_part[p] = stat_sum[p * block : (p + 1) * block].astype(bf16)
+        x, at = divmod(p * block, share)
+        stat_part[p] = stat_sum[x, at : at + block].astype(bf16)
     for j, peer in enumerate(ranks):
         to(
             {"dp": peer}, stat_part.at[peer], stat_recv.at[my_rank], st_sem.at[0], st_sem.at[1]
@@ -593,7 +631,7 @@
     planes = rep // CORES
     share = query_count // planes
     vdim = up_value.shape[2]
-    split = width // 2 // 256 * 256
+    split = width // 3 // 256 * 256
     chunks = hidden_width // (512 if hidden_width % 512 == 0 else 128)
     dma = pltpu.SemaphoreType.DMA
     hbm = pl.BlockSpec(memory_space=pltpu.HBM)
@@ -623,7 +661,7 @@
             pltpu.VMEM((dp, CORES * cap * PAGE, CKV), bf16),
             pltpu.VMEM((dp, dp, block, CKV), bf16),
             pltpu.VMEM((dp, dp, block, CKV), bf16),
-            pltpu.VMEM((query_count, PAGE), f32),
+            pltpu.VMEM((planes, share, PAGE), f32),
             pltpu.VMEM((dp, block, PAGE), bf16),
             pltpu.VMEM((dp, block, PAGE), bf16),
             pltpu.VMEM((query_count, CKV), f32),

time: 38.7 us -> 37.9 us (0.979)
  Pallas kernels: 38 us -> 37.2 us
    pallas_call x1, Pallas kernels: 38 us -> 37.2 us  [layer(): pl.pallas_call(functools.partial(layer_kernel, dp, rep), out_shape=jax.Sh...]
where the time goes in v5:
time: 37.9 us; the launch traced here: 37.8 us
  Pallas kernels  37.2 us (98%)
  local copies, waits for them, and re-layouts  0.6 us (2%)
    pallas_call x1, Pallas kernels, layer(): pl.pallas_call(functools.partial(layer_kernel, dp, rep), out_shape=jax.Sh...  37.2 us

profile of v5, /device:TPU:0, one launch (start us, length us, event | category | flops | bytes accessed | tf_op | source)
XLA Modules:
  0.0 37.8 jit_solution(2233859255174085856)
XLA Ops:
  0.0 37.2 %shard_map.127 = bf16[2,1792]{1,0:T(2,128)(2,1)S(1)} custom-call(s32[4,12]{1,0:T(4,128)} %page_rank_hbm.1, s32[4,12]{1,0:T(4,128)} %page_index_hbm.1, s32[1,4]{1,0:T(1,128)} %bitcast.1, bf16[2,36864]{1,0:T(2,128)(2,1)} %queries_hbm.1, bf16[2,576]{1,0:T(2,128)(2,1)} %fresh_hbm.1, bf16[2,1792]{1,0:T(2,128)(2,1)} %residual_hbm.1, f32[1792]{0:T(1024)} %gain_hbm.1, ...), custom_call_target="tpu_custom_call" | custom-call | tf_op jit(solution)/shard_map/pallas_call | solution.py:638
  37.2 0.6 %copy.15 = bf16[2,1792]{1,0:T(2,128)(2,1)} copy(bf16[2,1792]{1,0:T(2,128)(2,1)S(1)} %shard_map.127) | data formatting | bytes 14336
